TPU v7x, 32 devices: a whole 2x2x4 slice. The times are simulated.
32 devices in a mesh: slab: 16 (over z, x, core), grp: 2 (over y).
Axes of the slice: x: 2, y: 2, z: 4, core: 2. Of those that a mesh axis runs over, the one named last changes fastest.
Arguments:
- capture: float32 [2, 262144], P(None, ('slab', 'grp')), may hold values from -6 to 6
- dropped: int32 [16], P('slab'), may hold values from 0 to 8191
Outputs:
- max_held: float32 [128, 128, 128], P('slab', 'grp')
- coherent: float32 [2, 128, 128, 128], P(None, 'slab', 'grp')
All inputs are finite; a program needn't handle non-finite values.
Results may differ from a plain program's by a relative error of at most 0.0001.
Values sent between devices are 32-bit elements; how exact they have to be, the bound alone decides.
A program may use at most 128 MiB of HBM per device.

v0:
```python
import functools
import math

import jax
import jax.numpy as jnp
import numpy as np
from jax import lax
from jax.experimental import pallas as pl
from jax.experimental.pallas import tpu as pltpu
from jax.sharding import PartitionSpec as P

NCH = 256
HOP = 64
KW = 128
LW = 128
Q = 128
BLOCKS = 2
LANES = 128


def split_np(table):
    hi = table.astype(jnp.bfloat16)
    lo = (table - hi.astype(np.float64)).astype(jnp.bfloat16)
    return jnp.asarray(hi), jnp.asarray(lo)


def split(values):
    hi = values.astype(jnp.bfloat16)
    lo = (values - hi.astype(jnp.float32)).astype(jnp.bfloat16)
    return hi, lo


def dft_tables():
    i = np.arange(NCH)
    w = 0.5 - 0.5 * np.cos(2.0 * np.pi * i / NCH)
    w = w / np.sqrt(np.sum(w * w))
    turns = (i[:, None] * i[None, :] % NCH) * (2.0 * np.pi / NCH)
    cos, sin = w[:, None] * np.cos(turns), w[:, None] * np.sin(turns)
    to_real = np.concatenate([cos, sin], 0)
    to_imag = np.concatenate([-sin, cos], 0)
    return to_real, to_imag


def dot3(a_hi, a_lo, b_hi, b_lo, dims):
    dot = functools.partial(
        lax.dot_general, dimension_numbers=(dims, ((), ())), preferred_element_type=jnp.float32
    )
    return dot(a_hi, b_hi) + dot(a_lo, b_hi) + dot(a_hi, b_lo)


def cos_turns(turns, period):
    v = (jnp.abs(turns.astype(jnp.float32) * (1.0 / period) - 0.5) - 0.25) * (2.0 * math.pi)
    v2 = v * v
    total = jnp.full_like(v, 1.0 / math.factorial(13))
    for order in (11, 9, 7, 5, 3, 1):
        sign = 1.0 if order % 4 == 1 else -1.0
        total = total * v2 + sign / math.factorial(order)
    return total * v


def rotation(turns, period):
    return cos_turns(turns & (period - 1), period), cos_turns((turns + period // 4) & (period - 1), period)


def flip(index, by, bits):
    total = 0
    for bit in range(bits):
        w = 2**bit
        total = total + ((index // w + by // w) % 2) * w
    return total


def surfaces(
    own_blk, own_info, ty_hi, ty_lo, tx_hi, tx_lo, held, coh,
    buf, infos, ext, *rest,
    slabs, groups, own_bins, own_w
):
    slots = rest[:4], rest[4:8]
    line_sem, x_sem, y_sem, diag_sem, fwd_sem, recv_sem, isend_sem, irecv_sem = rest[8:]
    slab, grp = lax.axis_index("slab"), lax.axis_index("grp")
    bits = slabs.bit_length() - 1
    line = slabs // 4
    rows = Q // 2
    local = own_blk.shape[1]
    period = Q * HOP
    last = groups - 1
    partner = (flip(slab, 1, bits), grp)
    beside = (flip(slab, 2, bits), grp)
    across = (slab, 1 - grp)

    barrier = pltpu.get_barrier_semaphore()

    def greet(i, carry):
        pl.semaphore_signal(
            barrier,
            inc=1,
            device_id=(flip(slab, i // groups, bits), (grp + i) % groups),
            device_id_type=pl.DeviceIdType.MESH,
        )
        return carry

    lax.fori_loop(1, slabs * groups, greet, 0)

    def remote(src, dst, send, recv, target):
        return pltpu.make_async_remote_copy(
            src_ref=src, dst_ref=dst, send_sem=send, recv_sem=recv,
            device_id=target, device_id_type=pl.DeviceIdType.MESH,
        )

    def moved(k, dg, send, target, own=False):
        origin, g = flip(slab, k, bits), (grp + dg) % groups
        src = own_blk if own else buf.at[origin, g]
        return remote(src, buf.at[origin, g], send, recv_sem.at[origin, g], target)

    def arrived(k, dg):
        moved(k, dg, fwd_sem.at[0, 0, 0], partner).wait_recv()

    def info_copy(i):
        target = (flip(slab, i // groups, bits), (grp + i) % groups)
        return remote(own_info, infos.at[slab], isend_sem.at[i], irecv_sem.at[slab], target)

    def info_arrived(origin):
        remote(own_info, infos.at[origin], isend_sem.at[0], irecv_sem.at[origin], partner).wait_recv()

    def line_copy(kz):
        return moved(0, 0, line_sem.at[kz], (flip(slab, 4 * kz, bits), grp), True)

    def column_copies(kz, own=False):
        return [
            moved(4 * kz, 0, x_sem.at[kz], beside, own),
            moved(4 * kz, 0, y_sem.at[kz], across, own),
            moved(4 * kz, 0, fwd_sem.at[kz, 0, 0], partner, own),
        ]

    def forward(kz, kx, dg):
        return moved(4 * kz + 2 * kx, dg, fwd_sem.at[kz, kx, dg], partner)

    def diagonal_y(kz):
        return moved(4 * kz + 2, 0, diag_sem.at[kz], across)

    def diagonal_x(kz):
        return moved(4 * kz, 1, diag_sem.at[kz], beside)

    def from_line(kz):
        arrived(4 * kz, 0)
        for copy in column_copies(kz):
            copy.start()

    def from_x(kz):
        arrived(4 * kz + 2, 0)

        @pl.when(kz % 2 == 1)
        def _():
            diagonal_y(kz).start()

        forward(kz, 1, 0).start()

    def from_y(kz):
        arrived(4 * kz, 1)

        @pl.when(kz % 2 == 0)
        def _():
            diagonal_x(kz).start()

        forward(kz, 0, 1).start()

    def from_diagonal(kz):
        arrived(4 * kz + 2, 1)
        forward(kz, 1, 1).start()

    def run(first, end, act):
        def body(i, carry):
            act(i)
            return carry

        lax.fori_loop(first, end, body, 0)

    buf[slab, grp] = own_blk[...]
    held[...] = jnp.zeros_like(held)
    coh[...] = jnp.zeros_like(coh)
    pl.semaphore_wait(barrier, slabs * groups - 1)

    @pl.when(grp == last)
    def _():
        infos[slab] = own_info[...]
        run(1, slabs * groups, lambda i: info_copy(i).start())

    for copy in column_copies(0, True):
        copy.start()
    run(1, line, lambda kz: line_copy(kz).start())
    zero = slab * 0
    from_x(zero)
    from_y(zero)
    run(1, slabs, lambda i: info_arrived(flip(slab, i, bits)))

    @pl.when(grp != last)
    def _():
        info_arrived(slab)

    lane = lax.broadcasted_iota(jnp.int32, (rows, LANES), 1)
    low = lane < HOP
    jlane = lax.broadcasted_iota(jnp.int32, (8, Q), 1)
    jlane = 2 * (jlane & (rows - 1)) + (jlane >= rows).astype(jnp.int32)
    bins = slab * own_bins + lax.broadcasted_iota(jnp.int32, (own_bins, Q), 0)
    kchan = grp * own_w + lax.broadcasted_iota(jnp.int32, (own_w, Q), 0)
    lchan = KW + lax.broadcasted_iota(jnp.int32, (8, LW), 1)
    jsub = 2 * lax.broadcasted_iota(jnp.int32, (8, LW), 0)

    def spread(array, count):
        return jnp.concatenate([array[:1]] * count, axis=0)

    def events(t):
        @pl.when((t % 2 == 0) & (t // 2 + 1 < line))
        def _():
            from_line(t // 2 + 1)

        @pl.when((t % 2 == 1) & (t >= 3) & (t // 2 < line))
        def _():
            from_y(t // 2)
            from_x(t // 2)

        @pl.when((t % 3 == 2) & (t // 3 < line))
        def _():
            from_diagonal(t // 3)

        @pl.when(t % 2 == 1)
        def _():
            arrived(t, 0)
            arrived(t, 1)

    def prepare(t, slot):
        n = flip(slab, t, bits)
        before = (n - 1 + slabs) % slabs
        a_hi, a_lo, w_hi, w_lo = slot
        drops = jnp.zeros((1, LANES), jnp.float32)
        for other in range(slabs):
            drops = drops + infos[other, 4:5, :] * jnp.where(other <= n, 1.0, 0.0)
        stamp = jnp.concatenate([drops.astype(jnp.int32) + n * (BLOCKS * period)] * 8, axis=0)
        at_j = stamp + HOP * jlane
        phq = rotation(bins * (spread(at_j, own_bins) & (period - 1)), period)
        phx = rotation(kchan * (spread(at_j, own_w) & (NCH - 1)), NCH)
        phy = [rotation(lchan * ((stamp + HOP * (jsub + p)) & (NCH - 1)), NCH) for p in range(2)]

        for c in range(2):
            ext[c, 6:8, :] = infos[before, 2 * c : 2 * c + 2, :] * jnp.where(n > 0, 1.0, 0.0)
        for g in range(groups):
            ext[:, 8 + g * local : 8 + (g + 1) * local, :] = buf[n, g]
        frames_hi, frames_lo = [], []
        for b in range(BLOCKS):
            at = 8 + b * rows
            even, odd = [], []
            for c in range(2):
                r0 = ext[c, at : at + rows, :]
                r1 = ext[c, at - 1 : at - 1 + rows, :]
                r2 = ext[c, at - 2 : at - 2 + rows, :]
                even += [
                    pltpu.roll(jnp.where(low, r1, r2), HOP, 1),
                    pltpu.roll(jnp.where(low, r0, r1), HOP, 1),
                ]
                odd += [r1, r0]
            for part in (even, odd):
                hi, lo = split(jnp.concatenate(part, axis=1))
                frames_hi.append(hi)
                frames_lo.append(lo)
        f_hi = jnp.concatenate(frames_hi, axis=0)
        f_lo = jnp.concatenate(frames_lo, axis=0)
        upper = dot3(f_hi, f_lo, ty_hi[...], ty_lo[...], ((1,), (0,)))
        lower = dot3(tx_hi[...], tx_lo[...], f_hi, f_lo, ((1,), (1,)))

        phy_c = [jnp.concatenate([phy[p][0]] * (rows // 8), axis=0) for p in range(2)]
        phy_s = [jnp.concatenate([phy[p][1]] * (rows // 8), axis=0) for p in range(2)]
        for b in range(BLOCKS):
            zrs, zis = [], []
            for p in range(2):
                part = upper[(2 * b + p) * rows : (2 * b + p + 1) * rows]
                yr, yi = part[:, :LW], part[:, LW:]
                zrs.append(yr * phy_c[p] - yi * phy_s[p])
                zis.append(yr * phy_s[p] + yi * phy_c[p])
            zr_hi, zr_lo = split(jnp.concatenate(zrs, axis=0))
            zi_hi, zi_lo = split(jnp.concatenate(zis, axis=0))

            def weights(zr, zi):
                return jnp.concatenate(
                    [jnp.concatenate([zr, -zi], 1), jnp.concatenate([zi, zr], 1)], axis=0
                )

            w_hi[b] = weights(zr_hi, zi_hi)
            w_lo[b] = weights(zr_lo, zi_lo)
            xr = lower[:own_w, b * Q : (b + 1) * Q]
            xi = lower[own_w:, b * Q : (b + 1) * Q]
            ur = xr * phx[0] - xi * phx[1]
            ui = xr * phx[1] + xi * phx[0]
            for q in range(own_bins):
                c = phq[0][q : q + 1, :]
                s = phq[1][q : q + 1, :]
                hi, lo = split(jnp.concatenate([ur * c - ui * s, ur * s + ui * c], axis=1))
                a_hi[b, q * own_w : (q + 1) * own_w, :] = hi
                a_lo[b, q * own_w : (q + 1) * own_w, :] = lo

    def accumulate(slot):
        a_hi, a_lo, w_hi, w_lo = slot
        surf = [dot3(a_hi[b], a_lo[b], w_hi[b], w_lo[b], ((1,), (0,))) for b in range(BLOCKS)]
        largest, real, imag = held[...], coh[0], coh[1]
        for part in surf:
            sr = part[:, :LW].reshape(own_bins, own_w, LW)
            si = part[:, LW:].reshape(own_bins, own_w, LW)
            real, imag = real + sr, imag + si
            largest = jnp.maximum(largest, sr * sr + si * si)
        held[...] = largest
        coh[0] = real
        coh[1] = imag

    def pair(i, carry):
        t = 2 * i
        events(t + 1)
        prepare(t + 1, slots[1])
        accumulate(slots[0])
        events(t + 2)
        prepare(t + 2, slots[0])
        accumulate(slots[1])
        return carry

    events(zero)
    prepare(zero, slots[0])
    lax.fori_loop(0, slabs // 2 - 1, pair, 0)
    events(zero + slabs - 1)
    prepare(zero + slabs - 1, slots[1])
    accumulate(slots[0])
    accumulate(slots[1])
    held[...] = jnp.sqrt(held[...])
    coh[...] = coh[...] * (1.0 / math.sqrt(slabs * BLOCKS))

    @pl.when(grp == last)
    def _():
        run(1, slabs * groups, lambda i: info_copy(i).wait_send())

    run(1, line, lambda kz: line_copy(kz).wait_send())

    def sent(kz):
        for copy in column_copies(kz):
            copy.wait_send()
        diagonal_x(kz).wait_send()
        for kx, dg in ((0, 1), (1, 0), (1, 1)):
            forward(kz, kx, dg).wait_send()

    run(0, line, sent)


def on_device(capture, dropped):
    slabs = lax.axis_size("slab")
    groups = lax.axis_size("grp")
    grp = lax.axis_index("grp")
    own_bins = Q // slabs
    own_w = KW // groups
    local = capture.shape[1] // LANES
    to_real, to_imag = dft_tables()
    ty = np.concatenate([to_real[:, KW:], to_imag[:, KW:]], 1)
    tx = np.stack(
        [
            np.concatenate(
                [to_real[:, g * own_w : (g + 1) * own_w], to_imag[:, g * own_w : (g + 1) * own_w]], 1
            ).T
            for g in range(groups)
        ]
    ) / math.sqrt(Q)
    ty_hi, ty_lo = split_np(ty)
    tx_hi, tx_lo = (lax.dynamic_index_in_dim(t, grp, 0, False) for t in split_np(tx))
    blocks = capture.reshape(2, local, LANES)
    tail = capture[:, capture.shape[1] - 2 * LANES :].reshape(4, LANES)
    drop = jnp.broadcast_to(dropped.astype(jnp.float32).reshape(1, 1), (4, LANES))
    info = jnp.concatenate([tail, drop], axis=0)
    dma = pltpu.SemaphoreType.DMA
    slot = [pltpu.VMEM((BLOCKS, own_bins * own_w, 2 * Q), jnp.bfloat16)] * 2
    slot = slot + [pltpu.VMEM((BLOCKS, 2 * Q, 2 * LW), jnp.bfloat16)] * 2
    held, coherent = pl.pallas_call(
        functools.partial(surfaces, slabs=slabs, groups=groups, own_bins=own_bins, own_w=own_w),
        out_shape=[
            jax.ShapeDtypeStruct((own_bins, own_w, LW), jnp.float32),
            jax.ShapeDtypeStruct((2, own_bins, own_w, LW), jnp.float32),
        ],
        in_specs=[pl.BlockSpec(memory_space=pltpu.VMEM)] * 6,
        out_specs=[pl.BlockSpec(memory_space=pltpu.VMEM)] * 2,
        scratch_shapes=[
            pltpu.VMEM((slabs, groups, 2, local, LANES), jnp.float32),
            pltpu.VMEM((slabs, 8, LANES), jnp.float32),
            pltpu.VMEM((2, 8 + BLOCKS * Q // 2, LANES), jnp.float32),
            *slot,
            *slot,
            dma((slabs // 4,)),
            dma((slabs // 4,)),
            dma((slabs // 4,)),
            dma((slabs // 4,)),
            dma((slabs // 4, 2, groups)),
            dma((slabs, groups)),
            dma((slabs * groups,)),
            dma((slabs,)),
        ],
        compiler_params=pltpu.CompilerParams(
            collective_id=0, has_side_effects=True, vmem_limit_bytes=48 * 2**20
        ),
    )(
        blocks,
        info,
        ty_hi, ty_lo, tx_hi, tx_lo,
    )
    return held, coherent


def solution(mesh):
    in_specs = (P(None, ("slab", "grp")), P("slab"))
    out_specs = (P("slab", "grp", None), P(None, "slab", "grp", None))
    return jax.shard_map(
        on_device, mesh=mesh, in_specs=in_specs, out_specs=out_specs, check_vma=False
    )
```

profile of v0, /device:TPU:0, one launch (start us, length us, event | category | flops | bytes accessed | tf_op | source)
XLA Modules:
  0.0 43.2 jit_solution(18326588301311979411)
XLA Ops:
  1.3 0.7 %slice.3 = f32[2,256]{1,0:T(2,128)S(1)} slice(f32[2,8192]{1,0:T(2,128)} %param.6), slice={[0:2], [7936:8192]} | slice | bytes 4096 | tf_op jit(solution)/shard_map/slice | solution.py:369
  2.0 0.8 %copy.10 = f32[1,2,64,128]{3,2,1,0:T(8,128)S(1)} copy(f32[1,2,64,128]{3,1,2,0:T(2,128)} %bitcast.10) | data formatting | bytes 131072
  2.8 0.0 copy-start
  2.8 0.0 copy-start.1
  2.8 1.0 %dynamic-slice_bitcast_fusion = (bf16[128,512]{1,0:T(8,128)(2,1)S(1)}, bf16[128,512]{1,0:T(8,128)(2,1)S(1)}) fusion(bf16[2,128,512]{2,1,0:T(8,128)(2,1)} %constant.23.clone, s32[]{:T(128)S(6)} %select_n.5, bf16[2,128,512]{2,1,0:T(8,128)(2,1)} %constant.22.clone), kind=kLoop, calls=%fused_computation | loop fusion | bytes 524292 | tf_op jit(solution)/shard_map/jit(dynamic_index_in_dim)/squeeze | solution.py:367
  3.9 0.0 copy-done
  3.9 0.1 copy-done.1
  4.0 37.7 %shard_map.77 = (f32[8,64,128]{2,1,0:T(8,128)S(1)}, f32[2,8,64,128]{3,2,1,0:T(8,128)S(1)}) custom-call(f32[2,64,128]{2,1,0:T(8,128)S(1)} %bitcast.9, f32[8,128]{1,0:T(8,128)S(1)} %concatenate.3.own_info, bf16[512,256]{1,0:T(8,128)(2,1)S(1)} %copy-done.1, bf16[512,256]{1,0:T(8,128)(2,1)S(1)} %copy-done, bf16[128,512]{1,0:T(8,128)(2,1)S(1)} %get-tuple-element.3.tx_hi, ...), custom_call_target="tpu_custom_call" | custom-call | tf_op jit(solution)/shard_map/pallas_call | solution.py:375
  41.7 0.7 %copy.14 = f32[8,64,128]{2,1,0:T(8,128)} copy(f32[8,64,128]{2,1,0:T(8,128)S(1)} %get-tuple-element.6) | data formatting | bytes 524288
  42.4 0.8 %copy.15 = f32[2,8,64,128]{3,2,1,0:T(8,128)} copy(f32[2,8,64,128]{3,2,1,0:T(8,128)S(1)} %get-tuple-element.7) | data formatting | bytes 1048576
  (2 shorter events, 0.0 us)
Async XLA Ops:
  2.8 1.1 %copy-start = (bf16[512,256]{1,0:T(8,128)(2,1)S(1)}, bf16[512,256]{1,0:T(8,128)(2,1)}, u32[]{:S(2)}) copy-start(bf16[512,256]{1,0:T(8,128)(2,1)} %constant.21.clone.ty_lo) | copy-start | bytes 786436
  2.8 1.2 %copy-start.1 = (bf16[512,256]{1,0:T(8,128)(2,1)S(1)}, bf16[512,256]{1,0:T(8,128)(2,1)}, u32[]{:S(2)}) copy-start(bf16[512,256]{1,0:T(8,128)(2,1)} %constant.20.clone.ty_hi) | copy-start | bytes 786436
where the time goes:
time: 43.5 us; the launch traced here: 43.2 us
  Pallas kernels  37.7 us (87%)
  local copies, waits for them, and re-layouts  4.2 us (10%)
  between operations  1.3 us (3%)
    pallas_call x1, Pallas kernels, on_device(): pl.pallas_call(functools.partial(surfaces, slabs=slabs, groups=groups, ow...  37.7 us
    unnamed x7, local copies, waits for them, and re-layouts  2.44 us
    squeeze x1, local copies, waits for them, and re-layouts, on_device(): lax.dynamic_index_in_dim(t, grp, 0, False)  1.05 us

commit v1 on v0

v1 whole, which is shorter than its diff:
```python
import functools
import math

import jax
import jax.numpy as jnp
import numpy as np
from jax import lax
from jax.experimental import pallas as pl
from jax.experimental.pallas import tpu as pltpu
from jax.sharding import PartitionSpec as P

NCH = 256
HOP = 64
KW = 128
LW = 128
Q = 128
BLOCKS = 2
LANES = 128


def split_np(table):
    hi = table.astype(jnp.bfloat16)
    lo = (table - hi.astype(np.float64)).astype(jnp.bfloat16)
    return jnp.asarray(hi), jnp.asarray(lo)


def split(values):
    hi = values.astype(jnp.bfloat16)
    lo = (values - hi.astype(jnp.float32)).astype(jnp.bfloat16)
    return hi, lo


def dft_tables():
    i = np.arange(NCH)
    w = 0.5 - 0.5 * np.cos(2.0 * np.pi * i / NCH)
    w = w / np.sqrt(np.sum(w * w))
    turns = (i[:, None] * i[None, :] % NCH) * (2.0 * np.pi / NCH)
    cos, sin = w[:, None] * np.cos(turns), w[:, None] * np.sin(turns)
    to_real = np.concatenate([cos, sin], 0)
    to_imag = np.concatenate([-sin, cos], 0)
    return to_real, to_imag


def dot3(a_hi, a_lo, b_hi, b_lo, dims):
    dot = functools.partial(
        lax.dot_general, dimension_numbers=(dims, ((), ())), preferred_element_type=jnp.float32
    )
    return dot(a_hi, b_hi) + dot(a_lo, b_hi) + dot(a_hi, b_lo)


def cos_turns(turns, period):
    v = (jnp.abs(turns.astype(jnp.float32) * (1.0 / period) - 0.5) - 0.25) * (2.0 * math.pi)
    v2 = v * v
    total = jnp.full_like(v, 1.0 / math.factorial(13))
    for order in (11, 9, 7, 5, 3, 1):
        sign = 1.0 if order % 4 == 1 else -1.0
        total = total * v2 + sign / math.factorial(order)
    return total * v


def rotation(turns, period):
    return cos_turns(turns & (period - 1), period), cos_turns((turns + period // 4) & (period - 1), period)


def flip(index, by, bits):
    total = 0
    for bit in range(bits):
        w = 2**bit
        total = total + ((index // w + by // w) % 2) * w
    return total


def surfaces(
    own_blk, own_info, ty_hi, ty_lo, txs, tx_hi, held, coh,
    buf, infos, acc, got, ends, *rest,
    slabs, groups, own_bins, own_w
):
    slots = rest[:4], rest[4:8]
    line_sem, x_sem, y_sem, diag_sem, recv_sem, isend_sem, irecv_sem, swap_sem = rest[8:]
    slab, grp = lax.axis_index("slab"), lax.axis_index("grp")
    bits = slabs.bit_length() - 1
    line = slabs // 4
    rows = Q // 2
    bins = 2 * own_bins
    pairs = bins // 2
    period = Q * HOP
    last = groups - 1
    zero = slab * 0
    core = slab % 2
    chip = (slab // 2) % 2
    level = slab // 4
    partner = (slab + 1 - 2 * core, grp)
    beside = (slab + 2 - 4 * chip, grp)
    across = (slab, 1 - grp)

    barrier = pltpu.get_barrier_semaphore()

    def peer(i):
        return (flip(slab, i // groups, bits), (grp + i) % groups)

    def greet(i, carry):
        pl.semaphore_signal(
            barrier, inc=1, device_id=peer(i), device_id_type=pl.DeviceIdType.MESH
        )
        return carry

    lax.fori_loop(1, slabs * groups, greet, 0)

    def at_step(i):
        return jnp.where(i <= level, level - i, i)

    def remote(src, dst, send, recv, target):
        return pltpu.make_async_remote_copy(
            src_ref=src, dst_ref=dst, send_sem=send, recv_sem=recv,
            device_id=target, device_id_type=pl.DeviceIdType.MESH,
        )

    def moved(z, dx, dg, send, target, own=False):
        place = 2 * z + (chip + dx) % 2
        g = (grp + dg) % groups
        src = own_blk if own else buf.at[place, g]
        return remote(src, buf.at[place, g], send, recv_sem.at[place, g], target)

    def arrived(z, dx, dg):
        moved(z, dx, dg, line_sem.at[0], partner).wait_recv()

    def info_copy(i):
        return remote(own_info, infos.at[slab], isend_sem.at[i], irecv_sem.at[slab], peer(i))

    def info_arrived(origin):
        remote(own_info, infos.at[origin], isend_sem.at[0], irecv_sem.at[origin], partner).wait_recv()

    def line_copy(i):
        z = at_step(i)
        return moved(level, 0, 0, line_sem.at[i], (slab + 4 * (z - level), grp), True)

    def to_x(i, own=False):
        return moved(at_step(i), 0, 0, x_sem.at[i], beside, own)

    def to_y(i, own=False):
        return moved(at_step(i), 0, 0, y_sem.at[i], across, own)

    def diagonal(i):
        odd = i % 2
        dx, dg = odd, 1 - odd
        return dx, dg

    def diagonal_y(i):
        return moved(at_step(i), 1, 0, diag_sem.at[i], across)

    def diagonal_x(i):
        return moved(at_step(i), 0, 1, diag_sem.at[i], beside)

    def from_line(i):
        arrived(at_step(i), 0, 0)
        to_x(i).start()
        to_y(i).start()

    def from_sides(i):
        z = at_step(i)

        @pl.when(z % 2 == 1)
        def _():
            arrived(z, 1, 0)
            diagonal_y(i).start()
            arrived(z, 0, 1)

        @pl.when(z % 2 == 0)
        def _():
            arrived(z, 0, 1)
            diagonal_x(i).start()
            arrived(z, 1, 0)

    def run(first, end, act):
        def body(i, carry):
            act(i)
            return carry

        lax.fori_loop(first, end, body, 0)

    def reach(i):
        z = at_step(i)
        down = i <= level
        first = 4 * z - jnp.where(down & (z > 0), 1, 0)
        end = 4 * z + jnp.where(down & (i > 0), 3, 4)

        def wait(m):
            @pl.when((m != slab) | (grp != last))
            def _():
                info_arrived(m)

        run(first, end, wait)
        before = jnp.where(down, z + 1, z - 1)
        summed = jnp.where(down, z + 1, z)
        total = jnp.zeros((4, LANES), jnp.float32)
        for k in range(4):
            total = total + infos[4 * jnp.where(i == 0, z, summed) + k, 4:8, :] * jnp.where(
                (i > 0) | (4 * z + k > slab - core), 1.0, 0.0
            )
        base = ends[jnp.where(i == 0, z, before)] * jnp.where(i == 0, 0.0, 1.0)
        ends[z] = base + jnp.concatenate([total, total], axis=0) * jnp.where(down & (i > 0), -1.0, 1.0)

    buf[slab // 2, grp] = own_blk[...]
    acc[...] = jnp.zeros_like(acc)
    ends[...] = jnp.zeros_like(ends)
    pl.semaphore_wait(barrier, slabs * groups - 1)

    to_x(0, True).start()
    to_y(0, True).start()
    run(1, line, lambda i: line_copy(i).start())

    @pl.when(grp == last)
    def _():
        infos[slab] = own_info[...]
        run(1, slabs * groups, lambda i: info_copy(i).start())

    lane = lax.broadcasted_iota(jnp.int32, (rows, LANES), 1)
    low = lane < HOP
    jlane = lax.broadcasted_iota(jnp.int32, (16, Q), 1)
    jlane = 2 * (jlane & (rows - 1)) + (jlane >= rows).astype(jnp.int32)
    turn = lax.broadcasted_iota(jnp.int32, (16, Q), 0)
    turn = jnp.where(turn < 8, 2 * turn + 1, 2 * bins * (slab // 2) + bins - 1)
    lanes8 = lax.broadcasted_iota(jnp.int32, (8, LANES), 1)
    lchan = KW + lanes8
    kchan = grp * own_w + (lanes8 & (own_w - 1))
    ksign = jnp.where(lanes8 < own_w, -1.0, 1.0)
    jsub = 2 * lax.broadcasted_iota(jnp.int32, (8, LANES), 0)

    def spread(array, count):
        return jnp.concatenate([array] * count, axis=0)

    def events(u):
        i = u // 4

        @pl.when((u % 4 == 0) & (i < line))
        def _():
            reach(i)

        @pl.when((u % 2 == 1) & (u >= 3) & ((u + 3) // 2 < line))
        def _():
            from_line((u + 3) // 2)

        @pl.when((u % 2 == 1) & (u >= 5) & ((u - 1) // 2 < line))
        def _():
            from_sides((u - 1) // 2)

        @pl.when((u % 4 == 2) & (i < line))
        def _():
            arrived(at_step(i), 1, 1)

    def prepare(u, slot):
        z = at_step(u // 4)
        g = u % 2
        dx = (u // 2) % 2
        n = 4 * z + 2 * ((chip + dx) % 2) + core
        place = n // 2
        before = jnp.maximum(n - 1, 0)
        a_hi, a_lo, w_hi, w_lo = slot
        rel = ends[z]
        for k in range(1, 4):
            drop = infos[4 * z + k, 4:8, :] * jnp.where(4 * z + k > n, 1.0, 0.0)
            rel = rel - jnp.concatenate([drop, drop], axis=0)
        stamp = rel.astype(jnp.int32)
        t = (spread(stamp, 2) + HOP * jlane) & (period - 1)
        phq = rotation((turn * t) & (2 * period - 1), 2 * period)
        phx = [rotation(kchan * ((stamp + HOP * (jsub + p)) & (NCH - 1)), NCH) for p in range(2)]
        phy = [rotation(lchan * ((stamp + HOP * (jsub + p)) & (NCH - 1)), NCH) for p in range(2)]

        from_info = jnp.where((g == 0) & (n > 0), 1.0, 0.0)
        from_blk = jnp.where(g == 0, 0.0, 1.0)
        even, odd = [], []
        for c in range(2):
            base = c * rows
            tail = infos[before, 2 * c : 2 * c + 2, :] * from_info
            tail = tail + buf[place, 0, base + rows - 2 : base + rows, :] * from_blk
            r0 = buf[place, g, base : base + rows, :]
            r1 = jnp.concatenate([tail[1:2], buf[place, g, base : base + rows - 1, :]], axis=0)
            r2 = jnp.concatenate([tail, buf[place, g, base : base + rows - 2, :]], axis=0)
            even += [
                pltpu.roll(jnp.where(low, r1, r2), HOP, 1),
                pltpu.roll(jnp.where(low, r0, r1), HOP, 1),
            ]
            odd += [r1, r0]
        f_hi, f_lo = [], []
        for part in (even, odd):
            hi, lo = split(jnp.concatenate(part, axis=1))
            f_hi.append(hi)
            f_lo.append(lo)
        f_hi = jnp.concatenate(f_hi, axis=0)
        f_lo = jnp.concatenate(f_lo, axis=0)
        dot = functools.partial(jnp.dot, preferred_element_type=jnp.float32)
        upper = dot3(f_hi, f_lo, ty_hi[...], ty_lo[...], ((1,), (0,)))
        twice = dot(f_hi, txs[grp])
        lower = twice[:, :LANES] + dot(f_lo, tx_hi[grp]) + twice[:, LANES:]

        zrs, zis, kxs = [], [], []
        for p in range(2):
            c, s = (spread(v, rows // 8) for v in phy[p])
            part = upper[p * rows : (p + 1) * rows]
            yr, yi = part[:, :LW], part[:, LW:]
            zrs.append(yr * c - yi * s)
            zis.append(yr * s + yi * c)
            c, s = spread(phx[p][0], rows // 8), spread(phx[p][1] * ksign, rows // 8)
            part = lower[p * rows : (p + 1) * rows]
            kxs.append(part * c + pltpu.roll(part, own_w, 1) * s)
        zr_hi, zr_lo = split(jnp.concatenate(zrs, axis=0))
        zi_hi, zi_lo = split(jnp.concatenate(zis, axis=0))

        def weights(zr, zi):
            return jnp.concatenate(
                [jnp.concatenate([zr, -zi], 1), jnp.concatenate([zi, zr], 1)], axis=0
            )

        w_hi[...] = weights(zr_hi, zi_hi)
        w_lo[...] = weights(zr_lo, zi_lo)
        x = jnp.concatenate(kxs, axis=0).T
        xr, xi = x[:own_w], x[own_w:]
        c, s = phq[0][8:9], phq[1][8:9]
        ur = xr * c - xi * s
        ui = xr * s + xi * c

        def put(q, real, imag):
            hi, lo = split(jnp.concatenate([real, imag], axis=1))
            a_hi[q * own_w : (q + 1) * own_w, :] = hi
            a_lo[q * own_w : (q + 1) * own_w, :] = lo

        for m in range(pairs):
            c, s = phq[0][m : m + 1], phq[1][m : m + 1]
            rc, rs, ic, is_ = ur * c, ur * s, ui * c, ui * s
            put(pairs + m, rc - is_, ic + rs)
            put(pairs - 1 - m, rc + is_, ic - rs)

    def accumulate(slot, half):
        a_hi, a_lo, w_hi, w_lo = slot
        count = own_bins * own_w
        at = half * count if isinstance(half, int) else pl.multiple_of(half * count, count)
        part = dot3(
            a_hi[pl.ds(at, count), :], a_lo[pl.ds(at, count), :], w_hi[...], w_lo[...], ((1,), (0,))
        )
        sr = part[:, :LW].reshape(own_bins, own_w, LW)
        si = part[:, LW:].reshape(own_bins, own_w, LW)
        acc[half, 0] = jnp.maximum(acc[half, 0], sr * sr + si * si)
        acc[half, 1] = acc[half, 1] + sr
        acc[half, 2] = acc[half, 2] + si

    def both(slot):
        accumulate(slot, 0)
        accumulate(slot, 1)

    units = 4 * line

    def pair(i, carry):
        u = 2 * i
        events(u + 1)
        prepare(u + 1, slots[1])
        both(slots[0])
        events(u + 2)
        prepare(u + 2, slots[0])
        both(slots[1])
        return carry

    reach(zero)
    from_sides(zero)
    if line > 1:
        from_line(zero + 1)
    prepare(zero, slots[0])
    if line > 2:
        from_line(zero + 2)
    if line > 1:
        from_sides(zero + 1)
    lax.fori_loop(0, units // 2 - 1, pair, 0)
    prepare(zero + units - 1, slots[1])
    swap = remote(acc.at[1 - core], got, swap_sem.at[0], swap_sem.at[1], partner)
    accumulate(slots[0], 1 - core)
    accumulate(slots[1], 1 - core)
    swap.start()
    accumulate(slots[0], core)
    accumulate(slots[1], core)

    total = jnp.zeros((4, LANES), jnp.float32)
    for k in range(4):
        total = total + infos[k, 4:8, :]
    stamp = (jnp.concatenate([total, total], axis=0) - ends[0]).astype(jnp.int32) & (period - 1)
    klane = lax.broadcasted_iota(jnp.int32, (own_w, LANES), 1)
    ksub = grp * own_w + lax.broadcasted_iota(jnp.int32, (own_w, LANES), 0)
    kl = rotation((ksub - KW - klane) * spread(stamp, own_w // 8), NCH)
    qrow = slab * own_bins + lax.broadcasted_iota(jnp.int32, (8, LANES), 0)
    ql = rotation(qrow * stamp, period)
    scale = 1.0 / math.sqrt(slabs * BLOCKS)
    swap.wait_recv()
    held[...] = jnp.sqrt(jnp.maximum(acc[core, 0], got[0]))
    for q in range(own_bins):
        c, s = ql[0][q : q + 1] * scale, ql[1][q : q + 1] * scale
        fc = kl[0] * c - kl[1] * s
        fs = kl[0] * s + kl[1] * c
        real = acc[core, 1, q] + got[1, q]
        imag = acc[core, 2, q] + got[2, q]
        coh[0, q] = real * fc - imag * fs
        coh[1, q] = real * fs + imag * fc

    @pl.when(grp == last)
    def _():
        run(1, slabs * groups, lambda i: info_copy(i).wait_send())

    run(1, line, lambda i: line_copy(i).wait_send())

    def sent(i):
        to_x(i).wait_send()
        to_y(i).wait_send()
        diagonal_x(i).wait_send()

    run(0, line, sent)
    swap.wait_send()


def on_device(capture, dropped):
    slabs = lax.axis_size("slab")
    groups = lax.axis_size("grp")
    own_bins = Q // slabs
    own_w = KW // groups
    local = capture.shape[1] // LANES
    to_real, to_imag = dft_tables()
    ty = np.concatenate([to_real[:, KW:], to_imag[:, KW:]], 1)
    tx = np.stack(
        [
            np.concatenate(
                [to_real[:, g * own_w : (g + 1) * own_w], to_imag[:, g * own_w : (g + 1) * own_w]], 1
            )
            for g in range(groups)
        ]
    ) / math.sqrt(Q)
    ty_hi, ty_lo = split_np(ty)
    tx_hi, tx_lo = split_np(tx)
    txs = jnp.concatenate([tx_hi, tx_lo], axis=2)
    blocks = capture.reshape(2 * local, LANES)
    tail = capture[:, capture.shape[1] - 2 * LANES :].reshape(4, LANES)
    drop = jnp.broadcast_to(dropped.astype(jnp.float32).reshape(1, 1), (4, LANES))
    info = jnp.concatenate([tail, drop], axis=0)
    dma = pltpu.SemaphoreType.DMA
    line = slabs // 4
    count = 2 * own_bins * own_w
    slot = [pltpu.VMEM((count, 2 * Q), jnp.bfloat16)] * 2
    slot = slot + [pltpu.VMEM((2 * Q, 2 * LW), jnp.bfloat16)] * 2
    held, coherent = pl.pallas_call(
        functools.partial(surfaces, slabs=slabs, groups=groups, own_bins=own_bins, own_w=own_w),
        out_shape=[
            jax.ShapeDtypeStruct((own_bins, own_w, LW), jnp.float32),
            jax.ShapeDtypeStruct((2, own_bins, own_w, LW), jnp.float32),
        ],
        in_specs=[pl.BlockSpec(memory_space=pltpu.VMEM)] * 6,
        out_specs=[pl.BlockSpec(memory_space=pltpu.VMEM)] * 2,
        scratch_shapes=[
            pltpu.VMEM((slabs // 2, groups, 2 * local, LANES), jnp.float32),
            pltpu.VMEM((slabs, 8, LANES), jnp.float32),
            pltpu.VMEM((2, 3, own_bins, own_w, LW), jnp.float32),
            pltpu.VMEM((3, own_bins, own_w, LW), jnp.float32),
            pltpu.VMEM((line, 8, LANES), jnp.float32),
            *slot,
            *slot,
            dma((line,)),
            dma((line,)),
            dma((line,)),
            dma((line,)),
            dma((slabs // 2, groups)),
            dma((slabs * groups,)),
            dma((slabs,)),
            dma((2,)),
        ],
        compiler_params=pltpu.CompilerParams(
            collective_id=0, has_side_effects=True, vmem_limit_bytes=48 * 2**20
        ),
    )(
        blocks,
        info,
        ty_hi, ty_lo, txs, tx_hi,
    )
    return held, coherent


def solution(mesh):
    in_specs = (P(None, ("slab", "grp")), P("slab"))
    out_specs = (P("slab", "grp", None), P(None, "slab", "grp", None))
    return jax.shard_map(
        on_device, mesh=mesh, in_specs=in_specs, out_specs=out_specs, check_vma=False
    )
```

time: 43.5 us -> 47.5 us (1.092)
  the two profiles are of different devices: /device:TPU:0 before, /device:TPU:19 now
where the time goes in v1:
time: 47.5 us; the launch traced here: 47.2 us
  Pallas kernels  38.9 us (82%)
  local copies, waits for them, and re-layouts  6.98 us (15%)
  between operations  1.31 us (3%)
    pallas_call x1, Pallas kernels, on_device(): pl.pallas_call(functools.partial(surfaces, slabs=slabs, groups=groups, ow...  38.9 us
    unnamed x10, local copies, waits for them, and re-layouts  5.38 us

profile of v1, /device:TPU:19, one launch (start us, length us, event | category | flops | bytes accessed | tf_op | source)
XLA Modules:
  0.0 47.2 jit_solution(8524296927922992808)
XLA Ops:
  1.3 0.0 slice-start
  1.3 0.7 %slice-done = f32[2,256]{1,0:T(2,128)S(1)} async-done(((f32[2,8192]{1,0:T(2,128)}), f32[2,256]{1,0:T(2,128)S(1)}, s32[]{:S(2)}) %slice-start) | async-done | bytes 2072 | tf_op jit(solution)/shard_map/slice | solution.py:436
  2.0 0.9 %reshape.12.own_blk = f32[128,128]{1,0:T(8,128)S(1)} reshape(f32[2,8192]{1,0:T(2,128)} %param.6) | data formatting | bytes 131072 | tf_op jit(solution)/shard_map/reshape | solution.py:435
  2.9 0.0 copy-start
  2.9 1.0 %copy-done = bf16[2,512,256]{2,1,0:T(8,128)(2,1)S(1)} copy-done((bf16[2,512,256]{2,1,0:T(8,128)(2,1)S(1)}, bf16[2,512,256]{2,1,0:T(8,128)(2,1)}, u32[]{:S(2)}) %copy-start) | copy-done | bytes 524312
  3.9 0.0 copy-start.1
  3.9 0.9 %copy-done.1 = bf16[2,512,128]{2,1,0:T(8,128)(2,1)S(1)} copy-done((bf16[2,512,128]{2,1,0:T(8,128)(2,1)S(1)}, bf16[2,512,128]{2,1,0:T(8,128)(2,1)}, u32[]{:S(2)}) %copy-start.1) | copy-done | bytes 262168
  4.9 0.0 copy-start.2
  4.9 0.9 %copy-done.2 = bf16[512,256]{1,0:T(8,128)(2,1)S(1)} copy-done((bf16[512,256]{1,0:T(8,128)(2,1)S(1)}, bf16[512,256]{1,0:T(8,128)(2,1)}, u32[]{:S(2)}) %copy-start.2) | copy-done | bytes 262168
  5.8 0.0 copy-start.3
  5.8 0.9 %copy-done.3 = bf16[512,256]{1,0:T(8,128)(2,1)S(1)} copy-done((bf16[512,256]{1,0:T(8,128)(2,1)S(1)}, bf16[512,256]{1,0:T(8,128)(2,1)}, u32[]{:S(2)}) %copy-start.3) | copy-done | bytes 262168
  6.8 38.9 %shard_map.77 = (f32[8,64,128]{2,1,0:T(8,128)S(1)}, f32[2,8,64,128]{3,2,1,0:T(8,128)S(1)}) custom-call(f32[128,128]{1,0:T(8,128)S(1)} %reshape.12.own_blk, f32[8,128]{1,0:T(8,128)S(1)} %concatenate.6.own_info, bf16[512,256]{1,0:T(8,128)(2,1)S(1)} %copy-done.3, bf16[512,256]{1,0:T(8,128)(2,1)S(1)} %copy-done.2, bf16[2,512,256]{2,1,0:T(8,128)(2,1)S(1)} %copy-done, ...), custom_call_target="tpu_custom_call" | custom-call | tf_op jit(solution)/shard_map/pallas_call | solution.py:444
  45.7 0.7 %copy.11 = f32[8,64,128]{2,1,0:T(8,128)} copy(f32[8,64,128]{2,1,0:T(8,128)S(1)} %get-tuple-element.4) | data formatting | bytes 524288
  46.4 0.8 %copy.12 = f32[2,8,64,128]{3,2,1,0:T(8,128)} copy(f32[2,8,64,128]{3,2,1,0:T(8,128)S(1)} %get-tuple-element.5) | data formatting | bytes 1048576
  (2 shorter events, 0.0 us)
Async XLA Ops:
  1.3 0.7 %slice-start = ((f32[2,8192]{1,0:T(2,128)}), f32[2,256]{1,0:T(2,128)S(1)}, s32[]{:S(2)}) async-start(f32[2,8192]{1,0:T(2,128)} %param.6), calls=%async_computation | async-start | bytes 4096 | tf_op jit(solution)/shard_map/slice | solution.py:436
  2.9 1.0 %copy-start = (bf16[2,512,256]{2,1,0:T(8,128)(2,1)S(1)}, bf16[2,512,256]{2,1,0:T(8,128)(2,1)}, u32[]{:S(2)}) copy-start(bf16[2,512,256]{2,1,0:T(8,128)(2,1)} %constant.15.txs) | copy-start | bytes 1572868
  3.9 0.9 %copy-start.1 = (bf16[2,512,128]{2,1,0:T(8,128)(2,1)S(1)}, bf16[2,512,128]{2,1,0:T(8,128)(2,1)}, u32[]{:S(2)}) copy-start(bf16[2,512,128]{2,1,0:T(8,128)(2,1)} %constant.10.clone.tx_hi) | copy-start | bytes 786436
  4.9 0.9 %copy-start.2 = (bf16[512,256]{1,0:T(8,128)(2,1)S(1)}, bf16[512,256]{1,0:T(8,128)(2,1)}, u32[]{:S(2)}) copy-start(bf16[512,256]{1,0:T(8,128)(2,1)} %constant.9.clone.ty_lo) | copy-start | bytes 786436
  5.8 0.9 %copy-start.3 = (bf16[512,256]{1,0:T(8,128)(2,1)S(1)}, bf16[512,256]{1,0:T(8,128)(2,1)}, u32[]{:S(2)}) copy-start(bf16[512,256]{1,0:T(8,128)(2,1)} %constant.8.clone.ty_hi) | copy-start | bytes 786436

commit v2 on v1

--- a/solution.py
+++ b/solution.py
@@ -62,21 +62,13 @@
     return cos_turns(turns & (period - 1), period), cos_turns((turns + period // 4) & (period - 1), period)
 
 
-def flip(index, by, bits):
-    total = 0
-    for bit in range(bits):
-        w = 2**bit
-        total = total + ((index // w + by // w) % 2) * w
-    return total
-
-
 def surfaces(
-    own_blk, own_info, ty_hi, ty_lo, txs, tx_hi, held, coh,
-    buf, infos, acc, got, ends, *rest,
+    own_blk, own_info, ty_hbm, tx_hbm, held, coh,
+    buf, infos, acc, got, ends, ty, txs, *rest,
     slabs, groups, own_bins, own_w
 ):
     slots = rest[:4], rest[4:8]
-    line_sem, x_sem, y_sem, diag_sem, recv_sem, isend_sem, irecv_sem, swap_sem = rest[8:]
+    line_sem, x_sem, y_sem, diag_sem, recv_sem, isend_sem, irecv_sem, swap_sem, load_sem = rest[8:]
     slab, grp = lax.axis_index("slab"), lax.axis_index("grp")
     bits = slabs.bit_length() - 1
     line = slabs // 4
@@ -93,18 +85,33 @@
     beside = (slab + 2 - 4 * chip, grp)
     across = (slab, 1 - grp)
 
+    place = slab // 2
+
+    def load(src, dst, i):
+        return pltpu.make_async_copy(src, dst, load_sem.at[i])
+
+    tables = [load(ty_hbm, ty, 0), load(tx_hbm.at[grp], txs, 1)]
+    for copy in tables:
+        copy.start()
+
+    def chip_at(p):
+        return (2 * p + core, grp)
+
     barrier = pltpu.get_barrier_semaphore()
 
-    def peer(i):
-        return (flip(slab, i // groups, bits), (grp + i) % groups)
-
-    def greet(i, carry):
-        pl.semaphore_signal(
-            barrier, inc=1, device_id=peer(i), device_id_type=pl.DeviceIdType.MESH
-        )
-        return carry
-
-    lax.fori_loop(1, slabs * groups, greet, 0)
+    def greet(target):
+        pl.semaphore_signal(barrier, inc=1, device_id=target, device_id_type=pl.DeviceIdType.MESH)
+
+    def others(act):
+        def body(i, carry):
+            act((place + i) % (slabs // 2), i)
+            return carry
+
+        lax.fori_loop(1, slabs // 2, body, 0)
+
+    greet(partner)
+    greet(across)
+    others(lambda p, i: greet(chip_at(p)))
 
     def at_step(i):
         return jnp.where(i <= level, level - i, i)
@@ -115,35 +122,36 @@
             device_id=target, device_id_type=pl.DeviceIdType.MESH,
         )
 
-    def moved(z, dx, dg, send, target, own=False):
-        place = 2 * z + (chip + dx) % 2
+    def moved(z, dx, dg, send, target):
+        at = 2 * z + (chip + dx) % 2
         g = (grp + dg) % groups
-        src = own_blk if own else buf.at[place, g]
-        return remote(src, buf.at[place, g], send, recv_sem.at[place, g], target)
+        return remote(buf.at[at, g], buf.at[at, g], send, recv_sem.at[at, g], target)
 
     def arrived(z, dx, dg):
         moved(z, dx, dg, line_sem.at[0], partner).wait_recv()
 
-    def info_copy(i):
-        return remote(own_info, infos.at[slab], isend_sem.at[i], irecv_sem.at[slab], peer(i))
-
-    def info_arrived(origin):
-        remote(own_info, infos.at[origin], isend_sem.at[0], irecv_sem.at[origin], partner).wait_recv()
+    def info_copy(first, count, send, recv, target):
+        piece = infos.at[pl.ds(first, count)]
+        return remote(piece, piece, isend_sem.at[send], irecv_sem.at[recv], target)
+
+    chips = slabs // 2
+    to_group = info_copy(slab, 1, 0, 0, across)
+    to_partner = info_copy(slab, 1, chips, 1, partner)
+
+    def to_chip(p, i):
+        return info_copy(2 * place, 2, i, 2 + place, chip_at(p))
+
+    def info_arrived(p):
+        info_copy(2 * p, 2, 0, 2 + p, partner).wait_recv()
 
     def line_copy(i):
-        z = at_step(i)
-        return moved(level, 0, 0, line_sem.at[i], (slab + 4 * (z - level), grp), True)
-
-    def to_x(i, own=False):
-        return moved(at_step(i), 0, 0, x_sem.at[i], beside, own)
-
-    def to_y(i, own=False):
-        return moved(at_step(i), 0, 0, y_sem.at[i], across, own)
-
-    def diagonal(i):
-        odd = i % 2
-        dx, dg = odd, 1 - odd
-        return dx, dg
+        return moved(level, 0, 0, line_sem.at[i], (slab + 4 * (at_step(i) - level), grp))
+
+    def to_x(i):
+        return moved(at_step(i), 0, 0, x_sem.at[i], beside)
+
+    def to_y(i):
+        return moved(at_step(i), 0, 0, y_sem.at[i], across)
 
     def diagonal_y(i):
         return moved(at_step(i), 1, 0, diag_sem.at[i], across)
@@ -181,13 +189,13 @@
     def reach(i):
         z = at_step(i)
         down = i <= level
-        first = 4 * z - jnp.where(down & (z > 0), 1, 0)
-        end = 4 * z + jnp.where(down & (i > 0), 3, 4)
-
-        def wait(m):
-            @pl.when((m != slab) | (grp != last))
+        first = 2 * z - jnp.where(down & (z > 0), 1, 0)
+        end = 2 * z + jnp.where(down & (i > 0), 1, 2)
+
+        def wait(p):
+            @pl.when(p != place)
             def _():
-                info_arrived(m)
+                info_arrived(p)
 
         run(first, end, wait)
         before = jnp.where(down, z + 1, z - 1)
@@ -200,19 +208,32 @@
         base = ends[jnp.where(i == 0, z, before)] * jnp.where(i == 0, 0.0, 1.0)
         ends[z] = base + jnp.concatenate([total, total], axis=0) * jnp.where(down & (i > 0), -1.0, 1.0)
 
-    buf[slab // 2, grp] = own_blk[...]
+    own_load = load(own_blk, buf.at[place, grp], 2)
+    info_load = load(own_info, infos.at[slab], 3)
+    own_load.start()
+
+    @pl.when(grp == last)
+    def _():
+        info_load.start()
+
     acc[...] = jnp.zeros_like(acc)
     ends[...] = jnp.zeros_like(ends)
-    pl.semaphore_wait(barrier, slabs * groups - 1)
-
-    to_x(0, True).start()
-    to_y(0, True).start()
-    run(1, line, lambda i: line_copy(i).start())
+    own_load.wait()
 
     @pl.when(grp == last)
     def _():
-        infos[slab] = own_info[...]
-        run(1, slabs * groups, lambda i: info_copy(i).start())
+        info_load.wait()
+
+    pl.semaphore_wait(barrier, chips + 1)
+
+    @pl.when(grp == last)
+    def _():
+        to_group.start()
+        to_partner.start()
+
+    to_x(0).start()
+    to_y(0).start()
+    run(1, line, lambda i: line_copy(i).start())
 
     lane = lax.broadcasted_iota(jnp.int32, (rows, LANES), 1)
     low = lane < HOP
@@ -248,18 +269,22 @@
         def _():
             arrived(at_step(i), 1, 1)
 
-    def prepare(u, slot):
+    def prepare(u, slot, first=False):
         z = at_step(u // 4)
-        g = u % 2
+        g = 1 - u % 2
         dx = (u // 2) % 2
         n = 4 * z + 2 * ((chip + dx) % 2) + core
-        place = n // 2
+        at = n // 2
         before = jnp.maximum(n - 1, 0)
         a_hi, a_lo, w_hi, w_lo = slot
-        rel = ends[z]
-        for k in range(1, 4):
-            drop = infos[4 * z + k, 4:8, :] * jnp.where(4 * z + k > n, 1.0, 0.0)
-            rel = rel - jnp.concatenate([drop, drop], axis=0)
+        if first:
+            rel = infos[slab, 4:8, :] * jnp.where(core > 0, 1.0, 0.0)
+            rel = jnp.concatenate([rel, rel], axis=0)
+        else:
+            rel = ends[z]
+            for k in range(1, 4):
+                drop = infos[4 * z + k, 4:8, :] * jnp.where(4 * z + k > n, 1.0, 0.0)
+                rel = rel - jnp.concatenate([drop, drop], axis=0)
         stamp = rel.astype(jnp.int32)
         t = (spread(stamp, 2) + HOP * jlane) & (period - 1)
         phq = rotation((turn * t) & (2 * period - 1), 2 * period)
@@ -271,11 +296,12 @@
         even, odd = [], []
         for c in range(2):
             base = c * rows
-            tail = infos[before, 2 * c : 2 * c + 2, :] * from_info
-            tail = tail + buf[place, 0, base + rows - 2 : base + rows, :] * from_blk
-            r0 = buf[place, g, base : base + rows, :]
-            r1 = jnp.concatenate([tail[1:2], buf[place, g, base : base + rows - 1, :]], axis=0)
-            r2 = jnp.concatenate([tail, buf[place, g, base : base + rows - 2, :]], axis=0)
+            tail = buf[at, 0, base + rows - 2 : base + rows, :]
+            if not first:
+                tail = tail * from_blk + infos[before, 2 * c : 2 * c + 2, :] * from_info
+            r0 = buf[at, g, base : base + rows, :]
+            r1 = jnp.concatenate([tail[1:2], buf[at, g, base : base + rows - 1, :]], axis=0)
+            r2 = jnp.concatenate([tail, buf[at, g, base : base + rows - 2, :]], axis=0)
             even += [
                 pltpu.roll(jnp.where(low, r1, r2), HOP, 1),
                 pltpu.roll(jnp.where(low, r0, r1), HOP, 1),
@@ -289,9 +315,9 @@
         f_hi = jnp.concatenate(f_hi, axis=0)
         f_lo = jnp.concatenate(f_lo, axis=0)
         dot = functools.partial(jnp.dot, preferred_element_type=jnp.float32)
-        upper = dot3(f_hi, f_lo, ty_hi[...], ty_lo[...], ((1,), (0,)))
-        twice = dot(f_hi, txs[grp])
-        lower = twice[:, :LANES] + dot(f_lo, tx_hi[grp]) + twice[:, LANES:]
+        upper = dot3(f_hi, f_lo, ty[0], ty[1], ((1,), (0,)))
+        twice = dot(f_hi, txs[...])
+        lower = twice[:, :LANES] + dot(f_lo, txs[:, :LANES]) + twice[:, LANES:]
 
         zrs, zis, kxs = [], [], []
         for p in range(2):
@@ -359,16 +385,32 @@
         both(slots[1])
         return carry
 
-    reach(zero)
-    from_sides(zero)
+    @pl.when(grp != last)
+    def _():
+        to_group.wait_recv()
+        to_partner.start()
+
+    info_copy(slab + 1 - 2 * core, 1, 0, 1, partner).wait_recv()
+    others(lambda p, i: to_chip(p, i).start())
+    for copy in tables:
+        copy.wait()
     if line > 1:
         from_line(zero + 1)
-    prepare(zero, slots[0])
+    from_sides(zero)
+    prepare(zero, slots[0], True)
+    reach(zero)
     if line > 2:
         from_line(zero + 2)
+    prepare(zero + 1, slots[1])
+    accumulate(slots[0], 0)
+    accumulate(slots[0], 1)
+    arrived(at_step(zero), 1, 1)
     if line > 1:
         from_sides(zero + 1)
-    lax.fori_loop(0, units // 2 - 1, pair, 0)
+    prepare(zero + 2, slots[0])
+    accumulate(slots[1], 0)
+    accumulate(slots[1], 1)
+    lax.fori_loop(1, units // 2 - 1, pair, 0)
     prepare(zero + units - 1, slots[1])
     swap = remote(acc.at[1 - core], got, swap_sem.at[0], swap_sem.at[1], partner)
     accumulate(slots[0], 1 - core)
@@ -400,8 +442,10 @@
 
     @pl.when(grp == last)
     def _():
-        run(1, slabs * groups, lambda i: info_copy(i).wait_send())
-
+        to_group.wait_send()
+
+    to_partner.wait_send()
+    others(lambda p, i: to_chip(p, i).wait_send())
     run(1, line, lambda i: line_copy(i).wait_send())
 
     def sent(i):
@@ -429,9 +473,8 @@
             for g in range(groups)
         ]
     ) / math.sqrt(Q)
-    ty_hi, ty_lo = split_np(ty)
-    tx_hi, tx_lo = split_np(tx)
-    txs = jnp.concatenate([tx_hi, tx_lo], axis=2)
+    ty = jnp.stack(split_np(ty))
+    txs = jnp.concatenate(split_np(tx), axis=2)
     blocks = capture.reshape(2 * local, LANES)
     tail = capture[:, capture.shape[1] - 2 * LANES :].reshape(4, LANES)
     drop = jnp.broadcast_to(dropped.astype(jnp.float32).reshape(1, 1), (4, LANES))
@@ -447,7 +490,7 @@
             jax.ShapeDtypeStruct((own_bins, own_w, LW), jnp.float32),
             jax.ShapeDtypeStruct((2, own_bins, own_w, LW), jnp.float32),
         ],
-        in_specs=[pl.BlockSpec(memory_space=pltpu.VMEM)] * 6,
+        in_specs=[pl.BlockSpec(memory_space=pltpu.HBM)] * 4,
         out_specs=[pl.BlockSpec(memory_space=pltpu.VMEM)] * 2,
         scratch_shapes=[
             pltpu.VMEM((slabs // 2, groups, 2 * local, LANES), jnp.float32),
@@ -455,6 +498,8 @@
             pltpu.VMEM((2, 3, own_bins, own_w, LW), jnp.float32),
             pltpu.VMEM((3, own_bins, own_w, LW), jnp.float32),
             pltpu.VMEM((line, 8, LANES), jnp.float32),
+            pltpu.VMEM(ty.shape, jnp.bfloat16),
+            pltpu.VMEM(txs.shape[1:], jnp.bfloat16),
             *slot,
             *slot,
             dma((line,)),
@@ -462,9 +507,10 @@
             dma((line,)),
             dma((line,)),
             dma((slabs // 2, groups)),
-            dma((slabs * groups,)),
-            dma((slabs,)),
+            dma((slabs // 2 + 1,)),
+            dma((slabs // 2 + 2,)),
             dma((2,)),
+            dma((4,)),
         ],
         compiler_params=pltpu.CompilerParams(
             collective_id=0, has_side_effects=True, vmem_limit_bytes=48 * 2**20
@@ -472,7 +518,8 @@
     )(
         blocks,
         info,
-        ty_hi, ty_lo, txs, tx_hi,
+        ty,
+        txs,
     )
     return held, coherent
 

time: 47.5 us -> 39.9 us (0.84)
  the two profiles are of different devices: /device:TPU:19 before, /device:TPU:0 now
where the time goes in v2:
time: 39.9 us; the launch traced here: 39.4 us
  Pallas kernels  32.9 us (82%)
  local copies, waits for them, and re-layouts  5.17 us (13%)
  between operations  1.31 us (3%)
    pallas_call x1, Pallas kernels, on_device(): pl.pallas_call(functools.partial(surfaces, slabs=slabs, groups=groups, ow...  32.9 us
    unnamed x6, local copies, waits for them, and re-layouts  3.58 us
    reshape x1, local copies, waits for them, and re-layouts, on_device(): blocks = capture.reshape(2 * local, LANES)  0.9 us

profile of v2, /device:TPU:0, one launch (start us, length us, event | category | flops | bytes accessed | tf_op | source)
XLA Modules:
  0.0 39.4 jit_solution(2612131357922600240)
XLA Ops:
  1.3 0.0 slice-start
  1.3 0.7 %slice-done = f32[2,256]{1,0:T(2,128)S(1)} async-done(((f32[2,8192]{1,0:T(2,128)}), f32[2,256]{1,0:T(2,128)S(1)}, s32[]{:S(2)}) %slice-start) | async-done | bytes 2072 | tf_op jit(solution)/shard_map/slice | solution.py:479
  2.0 0.9 %reshape.12.own_blk = f32[128,128]{1,0:T(8,128)S(1)} reshape(f32[2,8192]{1,0:T(2,128)} %param.6) | data formatting | bytes 131072 | tf_op jit(solution)/shard_map/reshape | solution.py:478
  2.9 0.0 copy-start
  2.9 1.0 %copy-done = bf16[2,512,256]{2,1,0:T(8,128)(2,1)S(1)} copy-done((bf16[2,512,256]{2,1,0:T(8,128)(2,1)S(1)}, bf16[2,512,256]{2,1,0:T(8,128)(2,1)}, u32[]{:S(2)}) %copy-start) | copy-done | bytes 524312
  3.9 0.0 copy-start.1
  3.9 1.0 %copy-done.1 = bf16[2,512,256]{2,1,0:T(8,128)(2,1)S(1)} copy-done((bf16[2,512,256]{2,1,0:T(8,128)(2,1)S(1)}, bf16[2,512,256]{2,1,0:T(8,128)(2,1)}, u32[]{:S(2)}) %copy-start.1) | copy-done | bytes 524312
  5.0 32.9 %shard_map.77 = (f32[8,64,128]{2,1,0:T(8,128)S(1)}, f32[2,8,64,128]{3,2,1,0:T(8,128)S(1)}) custom-call(f32[128,128]{1,0:T(8,128)S(1)} %reshape.12.own_blk, f32[8,128]{1,0:T(8,128)S(1)} %concatenate.6.own_info, bf16[2,512,256]{2,1,0:T(8,128)(2,1)S(1)} %copy-done.1, bf16[2,512,256]{2,1,0:T(8,128)(2,1)S(1)} %copy-done), custom_call_target="tpu_custom_call" | custom-call | tf_op jit(solution)/shard_map/pallas_call | solution.py:487
  37.9 0.7 %copy.11 = f32[8,64,128]{2,1,0:T(8,128)} copy(f32[8,64,128]{2,1,0:T(8,128)S(1)} %get-tuple-element.4) | data formatting | bytes 524288
  38.6 0.8 %copy.12 = f32[2,8,64,128]{3,2,1,0:T(8,128)} copy(f32[2,8,64,128]{3,2,1,0:T(8,128)S(1)} %get-tuple-element.5) | data formatting | bytes 1048576
  (2 shorter events, 0.0 us)
Async XLA Ops:
  1.3 0.7 %slice-start = ((f32[2,8192]{1,0:T(2,128)}), f32[2,256]{1,0:T(2,128)S(1)}, s32[]{:S(2)}) async-start(f32[2,8192]{1,0:T(2,128)} %param.6), calls=%async_computation | async-start | bytes 4096 | tf_op jit(solution)/shard_map/slice | solution.py:479
  2.9 1.0 %copy-start = (bf16[2,512,256]{2,1,0:T(8,128)(2,1)S(1)}, bf16[2,512,256]{2,1,0:T(8,128)(2,1)}, u32[]{:S(2)}) copy-start(bf16[2,512,256]{2,1,0:T(8,128)(2,1)} %constant.18.tx_hbm) | copy-start | bytes 1572868
  3.9 1.0 %copy-start.1 = (bf16[2,512,256]{2,1,0:T(8,128)(2,1)S(1)}, bf16[2,512,256]{2,1,0:T(8,128)(2,1)}, u32[]{:S(2)}) copy-start(bf16[2,512,256]{2,1,0:T(8,128)(2,1)} %constant.17.ty_hbm) | copy-start | bytes 1572868

commit v3 on v2

--- a/solution.py
+++ b/solution.py
@@ -16,6 +16,7 @@
 Q = 128
 BLOCKS = 2
 LANES = 128
+VMEM_LIMIT = 67043328 - 1100 * 2**10
 
 
 def split_np(table):
@@ -61,20 +62,21 @@
 def rotation(turns, period):
     return cos_turns(turns & (period - 1), period), cos_turns((turns + period // 4) & (period - 1), period)
 
-
 def surfaces(
-    own_blk, own_info, ty_hbm, tx_hbm, held, coh,
-    buf, infos, acc, got, ends, ty, txs, *rest,
+    own_hbm, own_drop, ty_hbm, tx_hbm, held, coh,
+    raw, buf, infos, acc, got, ends, ty, txs, *rest,
     slabs, groups, own_bins, own_w
 ):
-    slots = rest[:4], rest[4:8]
-    line_sem, x_sem, y_sem, diag_sem, recv_sem, isend_sem, irecv_sem, swap_sem, load_sem = rest[8:]
+    a_hi, a_lo, w_hi, w_lo, spec_y, spec_x = rest[:6]
+    line_sem, x_sem, y_sem, diag_sem, recv_sem, isend_sem, irecv_sem, swap_sem, load_sem = rest[6:]
     slab, grp = lax.axis_index("slab"), lax.axis_index("grp")
     bits = slabs.bit_length() - 1
     line = slabs // 4
     rows = Q // 2
     bins = 2 * own_bins
     pairs = bins // 2
+    cut = min(4, own_bins)
+    cuts = own_bins // cut
     period = Q * HOP
     last = groups - 1
     zero = slab * 0
@@ -90,6 +92,8 @@
     def load(src, dst, i):
         return pltpu.make_async_copy(src, dst, load_sem.at[i])
 
+    own_load = load(own_hbm, raw, 2)
+    own_load.start()
     tables = [load(ty_hbm, ty, 0), load(tx_hbm.at[grp], txs, 1)]
     for copy in tables:
         copy.start()
@@ -208,21 +212,22 @@
         base = ends[jnp.where(i == 0, z, before)] * jnp.where(i == 0, 0.0, 1.0)
         ends[z] = base + jnp.concatenate([total, total], axis=0) * jnp.where(down & (i > 0), -1.0, 1.0)
 
-    own_load = load(own_blk, buf.at[place, grp], 2)
-    info_load = load(own_info, infos.at[slab], 3)
-    own_load.start()
+    ends[...] = jnp.zeros_like(ends)
+    acc[...] = jnp.zeros_like(acc)
+    own_load.wait()
+    for c in range(2):
+        buf[place, grp, c * rows : (c + 1) * rows, :] = raw[:, c, :]
 
     @pl.when(grp == last)
     def _():
-        info_load.start()
-
-    acc[...] = jnp.zeros_like(acc)
-    ends[...] = jnp.zeros_like(ends)
-    own_load.wait()
-
-    @pl.when(grp == last)
-    def _():
-        info_load.wait()
+        infos[slab] = jnp.concatenate(
+            [
+                raw[rows - 2 :, 0, :],
+                raw[rows - 2 :, 1, :],
+                jnp.broadcast_to(own_drop[0].astype(jnp.float32), (4, LANES)),
+            ],
+            axis=0,
+        )
 
     pl.semaphore_wait(barrier, chips + 1)
 
@@ -265,32 +270,24 @@
         def _():
             from_sides((u - 1) // 2)
 
-        @pl.when((u % 4 == 2) & (i < line))
+        @pl.when(u % 4 == 2)
         def _():
             arrived(at_step(i), 1, 1)
 
-    def prepare(u, slot, first=False):
+        if line > 1:
+
+            @pl.when(u == 2)
+            def _():
+                from_sides(zero + 1)
+
+    def locate(u):
         z = at_step(u // 4)
-        g = 1 - u % 2
-        dx = (u // 2) % 2
-        n = 4 * z + 2 * ((chip + dx) % 2) + core
-        at = n // 2
+        n = 4 * z + 2 * ((chip + u // 2) % 2) + core
+        return z, n, n // 2, 1 - u % 2
+
+    def analyze(u, slot, first=False):
+        z, n, at, g = locate(u)
         before = jnp.maximum(n - 1, 0)
-        a_hi, a_lo, w_hi, w_lo = slot
-        if first:
-            rel = infos[slab, 4:8, :] * jnp.where(core > 0, 1.0, 0.0)
-            rel = jnp.concatenate([rel, rel], axis=0)
-        else:
-            rel = ends[z]
-            for k in range(1, 4):
-                drop = infos[4 * z + k, 4:8, :] * jnp.where(4 * z + k > n, 1.0, 0.0)
-                rel = rel - jnp.concatenate([drop, drop], axis=0)
-        stamp = rel.astype(jnp.int32)
-        t = (spread(stamp, 2) + HOP * jlane) & (period - 1)
-        phq = rotation((turn * t) & (2 * period - 1), 2 * period)
-        phx = [rotation(kchan * ((stamp + HOP * (jsub + p)) & (NCH - 1)), NCH) for p in range(2)]
-        phy = [rotation(lchan * ((stamp + HOP * (jsub + p)) & (NCH - 1)), NCH) for p in range(2)]
-
         from_info = jnp.where((g == 0) & (n > 0), 1.0, 0.0)
         from_blk = jnp.where(g == 0, 0.0, 1.0)
         even, odd = [], []
@@ -319,15 +316,34 @@
         twice = dot(f_hi, txs[...])
         lower = twice[:, :LANES] + dot(f_lo, txs[:, :LANES]) + twice[:, LANES:]
 
+        spec_y[slot] = upper
+        spec_x[slot] = lower
+
+    def build(u, slot, first=False):
+        z, n, at, g = locate(u)
+        if first:
+            rel = infos[slab, 4:8, :] * jnp.where(core > 0, 1.0, 0.0)
+            rel = jnp.concatenate([rel, rel], axis=0)
+        else:
+            rel = ends[z]
+            for k in range(1, 4):
+                drop = infos[4 * z + k, 4:8, :] * jnp.where(4 * z + k > n, 1.0, 0.0)
+                rel = rel - jnp.concatenate([drop, drop], axis=0)
+        stamp = rel.astype(jnp.int32)
+        t = (spread(stamp, 2) + HOP * jlane) & (period - 1)
+        phq = rotation((turn * t) & (2 * period - 1), 2 * period)
+        phx = [rotation(kchan * ((stamp + HOP * (jsub + p)) & (NCH - 1)), NCH) for p in range(2)]
+        phy = [rotation(lchan * ((stamp + HOP * (jsub + p)) & (NCH - 1)), NCH) for p in range(2)]
+
         zrs, zis, kxs = [], [], []
         for p in range(2):
             c, s = (spread(v, rows // 8) for v in phy[p])
-            part = upper[p * rows : (p + 1) * rows]
+            part = spec_y[slot, p * rows : (p + 1) * rows, :]
             yr, yi = part[:, :LW], part[:, LW:]
             zrs.append(yr * c - yi * s)
             zis.append(yr * s + yi * c)
             c, s = spread(phx[p][0], rows // 8), spread(phx[p][1] * ksign, rows // 8)
-            part = lower[p * rows : (p + 1) * rows]
+            part = spec_x[slot, p * rows : (p + 1) * rows, :]
             kxs.append(part * c + pltpu.roll(part, own_w, 1) * s)
         zr_hi, zr_lo = split(jnp.concatenate(zrs, axis=0))
         zi_hi, zi_lo = split(jnp.concatenate(zis, axis=0))
@@ -337,8 +353,8 @@
                 [jnp.concatenate([zr, -zi], 1), jnp.concatenate([zi, zr], 1)], axis=0
             )
 
-        w_hi[...] = weights(zr_hi, zi_hi)
-        w_lo[...] = weights(zr_lo, zi_lo)
+        w_hi[slot] = weights(zr_hi, zi_hi)
+        w_lo[slot] = weights(zr_lo, zi_lo)
         x = jnp.concatenate(kxs, axis=0).T
         xr, xi = x[:own_w], x[own_w:]
         c, s = phq[0][8:9], phq[1][8:9]
@@ -347,42 +363,42 @@
 
         def put(q, real, imag):
             hi, lo = split(jnp.concatenate([real, imag], axis=1))
-            a_hi[q * own_w : (q + 1) * own_w, :] = hi
-            a_lo[q * own_w : (q + 1) * own_w, :] = lo
-
-        for m in range(pairs):
-            c, s = phq[0][m : m + 1], phq[1][m : m + 1]
-            rc, rs, ic, is_ = ur * c, ur * s, ui * c, ui * s
-            put(pairs + m, rc - is_, ic + rs)
-            put(pairs - 1 - m, rc + is_, ic - rs)
-
-    def accumulate(slot, half):
-        a_hi, a_lo, w_hi, w_lo = slot
-        count = own_bins * own_w
-        at = half * count if isinstance(half, int) else pl.multiple_of(half * count, count)
-        part = dot3(
-            a_hi[pl.ds(at, count), :], a_lo[pl.ds(at, count), :], w_hi[...], w_lo[...], ((1,), (0,))
-        )
-        sr = part[:, :LW].reshape(own_bins, own_w, LW)
-        si = part[:, LW:].reshape(own_bins, own_w, LW)
-        acc[half, 0] = jnp.maximum(acc[half, 0], sr * sr + si * si)
-        acc[half, 1] = acc[half, 1] + sr
-        acc[half, 2] = acc[half, 2] + si
-
-    def both(slot):
+            a_hi[slot, q * own_w : (q + 1) * own_w, :] = hi
+            a_lo[slot, q * own_w : (q + 1) * own_w, :] = lo
+
+        def turned(c):
+            for m in range(c * cut // 2, (c + 1) * cut // 2):
+                c, s = phq[0][m : m + 1], phq[1][m : m + 1]
+                rc, rs, ic, is_ = ur * c, ur * s, ui * c, ui * s
+                put(pairs + m, rc - is_, ic + rs)
+                put(pairs - 1 - m, rc + is_, ic - rs)
+
+        return turned
+
+    def accumulate(slot, c):
+        count = cut * own_w
+        at = pl.ds(c * count if isinstance(c, int) else pl.multiple_of(c * count, count), count)
+        part = dot3(a_hi[slot, at, :], a_lo[slot, at, :], w_hi[slot], w_lo[slot], ((1,), (0,)))
+        sr = part[:, :LW].reshape(cut, own_w, LW)
+        si = part[:, LW:].reshape(cut, own_w, LW)
+        half, piece = c // cuts, c % cuts
+        q = pl.ds(piece * cut, cut)
+        acc[half, 0, q] = jnp.maximum(acc[half, 0, q], sr * sr + si * si)
+        acc[half, 1, q] = acc[half, 1, q] + sr
+        acc[half, 2, q] = acc[half, 2, q] + si
+
+    units = 4 * line
+
+    def step(u, carry):
+        slot = u % 2
+        events(u + 2)
         accumulate(slot, 0)
-        accumulate(slot, 1)
-
-    units = 4 * line
-
-    def pair(i, carry):
-        u = 2 * i
-        events(u + 1)
-        prepare(u + 1, slots[1])
-        both(slots[0])
-        events(u + 2)
-        prepare(u + 2, slots[0])
-        both(slots[1])
+        turned = build(u + 1, 1 - slot)
+        analyze(u + 2, slot)
+        turned(0)
+        for c in range(1, 2 * cuts):
+            accumulate(slot, c)
+            turned(c)
         return carry
 
     @pl.when(grp != last)
@@ -397,27 +413,35 @@
     if line > 1:
         from_line(zero + 1)
     from_sides(zero)
-    prepare(zero, slots[0], True)
+    analyze(zero, 0, True)
     reach(zero)
     if line > 2:
         from_line(zero + 2)
-    prepare(zero + 1, slots[1])
-    accumulate(slots[0], 0)
-    accumulate(slots[0], 1)
-    arrived(at_step(zero), 1, 1)
-    if line > 1:
-        from_sides(zero + 1)
-    prepare(zero + 2, slots[0])
-    accumulate(slots[1], 0)
-    accumulate(slots[1], 1)
-    lax.fori_loop(1, units // 2 - 1, pair, 0)
-    prepare(zero + units - 1, slots[1])
-    swap = remote(acc.at[1 - core], got, swap_sem.at[0], swap_sem.at[1], partner)
-    accumulate(slots[0], 1 - core)
-    accumulate(slots[1], 1 - core)
-    swap.start()
-    accumulate(slots[0], core)
-    accumulate(slots[1], core)
+    turned = build(zero, 0, True)
+    analyze(zero + 1, 1)
+    for c in range(2 * cuts):
+        turned(c)
+    lax.fori_loop(0, units - 2, step, 0)
+    turned = build(zero + units - 1, 1)
+    for c in range(2 * cuts):
+        turned(c)
+    def swap(c):
+        q = pl.ds(c * cut, cut)
+        return [
+            remote(
+                acc.at[1 - core, k, q], got.at[k, q], swap_sem.at[0, 3 * c + k], swap_sem.at[1, 3 * c + k], partner
+            )
+            for k in range(3)
+        ]
+
+    for c in range(cuts):
+        for slot in range(2):
+            accumulate(slot, (1 - core) * cuts + c)
+        for copy in swap(c):
+            copy.start()
+    for c in range(cuts):
+        for slot in range(2):
+            accumulate(slot, core * cuts + c)
 
     total = jnp.zeros((4, LANES), jnp.float32)
     for k in range(4):
@@ -429,7 +453,9 @@
     qrow = slab * own_bins + lax.broadcasted_iota(jnp.int32, (8, LANES), 0)
     ql = rotation(qrow * stamp, period)
     scale = 1.0 / math.sqrt(slabs * BLOCKS)
-    swap.wait_recv()
+    for c in range(cuts):
+        for copy in swap(c):
+            copy.wait_recv()
     held[...] = jnp.sqrt(jnp.maximum(acc[core, 0], got[0]))
     for q in range(own_bins):
         c, s = ql[0][q : q + 1] * scale, ql[1][q : q + 1] * scale
@@ -454,7 +480,9 @@
         diagonal_x(i).wait_send()
 
     run(0, line, sent)
-    swap.wait_send()
+    for c in range(cuts):
+        for copy in swap(c):
+            copy.wait_send()
 
 
 def on_device(capture, dropped):
@@ -475,24 +503,23 @@
     ) / math.sqrt(Q)
     ty = jnp.stack(split_np(ty))
     txs = jnp.concatenate(split_np(tx), axis=2)
-    blocks = capture.reshape(2 * local, LANES)
-    tail = capture[:, capture.shape[1] - 2 * LANES :].reshape(4, LANES)
-    drop = jnp.broadcast_to(dropped.astype(jnp.float32).reshape(1, 1), (4, LANES))
-    info = jnp.concatenate([tail, drop], axis=0)
+    blocks = capture.reshape(2, local, LANES).transpose(1, 0, 2)
     dma = pltpu.SemaphoreType.DMA
     line = slabs // 4
     count = 2 * own_bins * own_w
-    slot = [pltpu.VMEM((count, 2 * Q), jnp.bfloat16)] * 2
-    slot = slot + [pltpu.VMEM((2 * Q, 2 * LW), jnp.bfloat16)] * 2
+    slot = [pltpu.VMEM((2, count, 2 * Q), jnp.bfloat16)] * 2
+    slot = slot + [pltpu.VMEM((2, 2 * Q, 2 * LW), jnp.bfloat16)] * 2
+    slot = slot + [pltpu.VMEM((2, Q, w), jnp.float32) for w in (2 * LW, LANES)]
     held, coherent = pl.pallas_call(
         functools.partial(surfaces, slabs=slabs, groups=groups, own_bins=own_bins, own_w=own_w),
         out_shape=[
             jax.ShapeDtypeStruct((own_bins, own_w, LW), jnp.float32),
             jax.ShapeDtypeStruct((2, own_bins, own_w, LW), jnp.float32),
         ],
-        in_specs=[pl.BlockSpec(memory_space=pltpu.HBM)] * 4,
+        in_specs=[pl.BlockSpec(memory_space=space) for space in (pltpu.HBM, pltpu.SMEM, pltpu.HBM, pltpu.HBM)],
         out_specs=[pl.BlockSpec(memory_space=pltpu.VMEM)] * 2,
         scratch_shapes=[
+            pltpu.VMEM((local, 2, LANES), jnp.float32),
             pltpu.VMEM((slabs // 2, groups, 2 * local, LANES), jnp.float32),
             pltpu.VMEM((slabs, 8, LANES), jnp.float32),
             pltpu.VMEM((2, 3, own_bins, own_w, LW), jnp.float32),
@@ -501,7 +528,6 @@
             pltpu.VMEM(ty.shape, jnp.bfloat16),
             pltpu.VMEM(txs.shape[1:], jnp.bfloat16),
             *slot,
-            *slot,
             dma((line,)),
             dma((line,)),
             dma((line,)),
@@ -509,15 +535,15 @@
             dma((slabs // 2, groups)),
             dma((slabs // 2 + 1,)),
             dma((slabs // 2 + 2,)),
-            dma((2,)),
-            dma((4,)),
+            dma((2, 3 * own_bins)),
+            dma((3,)),
         ],
         compiler_params=pltpu.CompilerParams(
-            collective_id=0, has_side_effects=True, vmem_limit_bytes=48 * 2**20
+            collective_id=0, has_side_effects=True, vmem_limit_bytes=VMEM_LIMIT
         ),
     )(
         blocks,
-        info,
+        dropped,
         ty,
         txs,
     )

time: 39.9 us -> 37.5 us (0.940)
  local copies, waits for them, and re-layouts: 5.17 us -> 2.53 us
  Pallas kernels: 32.9 us -> 33.3 us
    unnamed x6 -> x4, local copies, waits for them, and re-layouts: 3.58 us -> 2.53 us
    reshape x2 -> x0, local copies, waits for them, and re-layouts: 0.91 us -> none  [the longest x1 0.9 us: on_device(): blocks = capture.reshape(2 * local, LANES)]
    slice x2 -> x0, local copies, waits for them, and re-layouts: 0.68 us -> none  [on_device(): tail = capture[:, capture.shape[1] - 2 * LANES:].reshape(4, LANES)]
    pallas_call x1, Pallas kernels: 32.9 us -> 33.3 us  [on_device(): pl.pallas_call(functools.partial(surfaces, slabs=slabs, groups=groups, ow...]
where the time goes in v3:
time: 37.5 us; the launch traced here: 37.1 us
  Pallas kernels  33.3 us (89%)
  local copies, waits for them, and re-layouts  2.53 us (7%)
  between operations  1.29 us (3%)
    pallas_call x1, Pallas kernels, on_device(): pl.pallas_call(functools.partial(surfaces, slabs=slabs, groups=groups, ow...  33.3 us
    unnamed x4, local copies, waits for them, and re-layouts  2.53 us

profile of v3, /device:TPU:0, one launch (start us, length us, event | category | flops | bytes accessed | tf_op | source)
XLA Modules:
  0.0 37.1 jit_solution(7801382458255590635)
XLA Ops:
  1.3 33.3 %shard_map.77 = (f32[8,64,128]{2,1,0:T(8,128)}, f32[2,8,64,128]{3,2,1,0:T(8,128)}) custom-call(f32[64,2,128]{2,1,0:T(2,128)} %bitcast.3, s32[1]{0:T(128)S(6)} %copy.10.own_drop, bf16[2,512,256]{2,1,0:T(8,128)(2,1)} %constant.15.ty_hbm, bf16[2,512,256]{2,1,0:T(8,128)(2,1)} %constant.16.tx_hbm), custom_call_target="tpu_custom_call" | custom-call | tf_op jit(solution)/shard_map/pallas_call | solution.py:513
  34.6 0.0 copy-start
  34.6 1.7 %copy.11 = f32[8,64,128]{2,1,0:T(8,128)} copy(f32[8,64,128]{2,1,0:T(8,128)} %get-tuple-element.4) | data formatting | bytes 524288
  36.3 0.0 copy-done
  36.4 0.8 %copy.12 = f32[2,8,64,128]{3,2,1,0:T(8,128)} copy(f32[2,8,64,128]{3,2,1,0:T(8,128)S(1)} %copy-done) | data formatting | bytes 1048576
Async XLA Ops:
  34.6 1.7 %copy-start = (f32[2,8,64,128]{3,2,1,0:T(8,128)S(1)}, f32[2,8,64,128]{3,2,1,0:T(8,128)}, u32[]{:S(2)}) copy-start(f32[2,8,64,128]{3,2,1,0:T(8,128)} %get-tuple-element.5) | copy-start | bytes 1572868

commit v4 on v3

--- a/solution.py
+++ b/solution.py
@@ -16,7 +16,7 @@
 Q = 128
 BLOCKS = 2
 LANES = 128
-VMEM_LIMIT = 67043328 - 1100 * 2**10
+VMEM_LIMIT = 67043328 - 11300 * 2**10
 
 
 def split_np(table):
@@ -157,11 +157,9 @@
     def to_y(i):
         return moved(at_step(i), 0, 0, y_sem.at[i], across)
 
-    def diagonal_y(i):
-        return moved(at_step(i), 1, 0, diag_sem.at[i], across)
-
-    def diagonal_x(i):
-        return moved(at_step(i), 0, 1, diag_sem.at[i], beside)
+    def diagonal(i):
+        odd = at_step(i) % 2
+        return moved(at_step(i), odd, 1 - odd, diag_sem.at[i], (slab + (2 - 4 * chip) * (1 - odd), grp + odd * (1 - 2 * grp)))
 
     def from_line(i):
         arrived(at_step(i), 0, 0)
@@ -169,19 +167,10 @@
         to_y(i).start()
 
     def from_sides(i):
-        z = at_step(i)
-
-        @pl.when(z % 2 == 1)
-        def _():
-            arrived(z, 1, 0)
-            diagonal_y(i).start()
-            arrived(z, 0, 1)
-
-        @pl.when(z % 2 == 0)
-        def _():
-            arrived(z, 0, 1)
-            diagonal_x(i).start()
-            arrived(z, 1, 0)
+        odd = at_step(i) % 2
+        arrived(at_step(i), odd, 1 - odd)
+        diagonal(i).start()
+        arrived(at_step(i), 1 - odd, odd)
 
     def run(first, end, act):
         def body(i, carry):
@@ -255,30 +244,30 @@
     def spread(array, count):
         return jnp.concatenate([array] * count, axis=0)
 
-    def events(u):
-        i = u // 4
-
-        @pl.when((u % 4 == 0) & (i < line))
-        def _():
-            reach(i)
-
-        @pl.when((u % 2 == 1) & (u >= 3) & ((u + 3) // 2 < line))
-        def _():
-            from_line((u + 3) // 2)
-
-        @pl.when((u % 2 == 1) & (u >= 5) & ((u - 1) // 2 < line))
-        def _():
-            from_sides((u - 1) // 2)
-
-        @pl.when(u % 4 == 2)
-        def _():
+    def events(i, w):
+        if w == 0:
             arrived(at_step(i), 1, 1)
 
-        if line > 1:
-
-            @pl.when(u == 2)
+            @pl.when((i == 0) & (line > 1))
             def _():
-                from_sides(zero + 1)
+                from_sides(i + 1)
+
+        elif w == 2:
+
+            @pl.when(i + 1 < line)
+            def _():
+                reach(i + 1)
+
+        else:
+            j = 2 * i + (w + 1) // 2
+
+            @pl.when(j + 2 < line)
+            def _():
+                from_line(j + 2)
+
+            @pl.when((j > 1) & (j < line))
+            def _():
+                from_sides(j)
 
     def locate(u):
         z = at_step(u // 4)
@@ -313,11 +302,14 @@
         f_lo = jnp.concatenate(f_lo, axis=0)
         dot = functools.partial(jnp.dot, preferred_element_type=jnp.float32)
         upper = dot3(f_hi, f_lo, ty[0], ty[1], ((1,), (0,)))
-        twice = dot(f_hi, txs[...])
-        lower = twice[:, :LANES] + dot(f_lo, txs[:, :LANES]) + twice[:, LANES:]
 
         spec_y[slot] = upper
-        spec_x[slot] = lower
+
+        def finish():
+            twice = dot(f_hi, txs[...])
+            spec_x[slot] = twice[:, :LANES] + dot(f_lo, txs[:, :LANES]) + twice[:, LANES:]
+
+        return finish
 
     def build(u, slot, first=False):
         z, n, at, g = locate(u)
@@ -375,10 +367,19 @@
 
         return turned
 
-    def accumulate(slot, c):
+    def accumulate(slot, c, late):
         count = cut * own_w
         at = pl.ds(c * count if isinstance(c, int) else pl.multiple_of(c * count, count), count)
-        part = dot3(a_hi[slot, at, :], a_lo[slot, at, :], w_hi[slot], w_lo[slot], ((1,), (0,)))
+        hi = a_hi[slot, at, :]
+        dot = functools.partial(jnp.dot, preferred_element_type=jnp.float32)
+        both = jnp.concatenate([hi, a_lo[slot, at, :]], axis=0)
+        if late:
+            once = dot(hi, w_lo[slot])
+            twice = dot(both, w_hi[slot])
+        else:
+            twice = dot(both, w_hi[slot])
+            once = dot(hi, w_lo[slot])
+        part = twice[:count] + twice[count:] + once
         sr = part[:, :LW].reshape(cut, own_w, LW)
         si = part[:, LW:].reshape(cut, own_w, LW)
         half, piece = c // cuts, c % cuts
@@ -389,17 +390,25 @@
 
     units = 4 * line
 
-    def step(u, carry):
+    def step(i, w, slot):
+        u = 4 * i + w
         slot = u % 2
-        events(u + 2)
-        accumulate(slot, 0)
+        events(i, w)
+        accumulate(slot, 0, 0)
         turned = build(u + 1, 1 - slot)
-        analyze(u + 2, slot)
+        finish = analyze(u + 2, slot)
         turned(0)
         for c in range(1, 2 * cuts):
-            accumulate(slot, c)
+            accumulate(slot, c, c % 2)
+            if c == 1:
+                finish()
             turned(c)
-        return carry
+        return 1 - slot
+
+    def steps(i, slot):
+        for w in range(4):
+            slot = step(i, w, slot)
+        return slot
 
     @pl.when(grp != last)
     def _():
@@ -413,16 +422,19 @@
     if line > 1:
         from_line(zero + 1)
     from_sides(zero)
-    analyze(zero, 0, True)
+    analyze(zero, 0, True)()
     reach(zero)
     if line > 2:
         from_line(zero + 2)
     turned = build(zero, 0, True)
-    analyze(zero + 1, 1)
+    analyze(zero + 1, 1)()
     for c in range(2 * cuts):
         turned(c)
-    lax.fori_loop(0, units - 2, step, 0)
-    turned = build(zero + units - 1, 1)
+    slot = lax.fori_loop(0, line - 1, steps, zero)
+    slot = step(zero + line - 1, 0, slot)
+    step(zero + line - 1, 1, slot)
+    slot = 0
+    turned = build(zero + units - 1, 1 - slot)
     for c in range(2 * cuts):
         turned(c)
     def swap(c):
@@ -435,13 +447,13 @@
         ]
 
     for c in range(cuts):
-        for slot in range(2):
-            accumulate(slot, (1 - core) * cuts + c)
+        for late, other in enumerate((slot, 1 - slot)):
+            accumulate(other, (1 - core) * cuts + c, late)
         for copy in swap(c):
             copy.start()
     for c in range(cuts):
-        for slot in range(2):
-            accumulate(slot, core * cuts + c)
+        for late, other in enumerate((slot, 1 - slot)):
+            accumulate(other, core * cuts + c, late)
 
     total = jnp.zeros((4, LANES), jnp.float32)
     for k in range(4):
@@ -477,12 +489,23 @@
     def sent(i):
         to_x(i).wait_send()
         to_y(i).wait_send()
-        diagonal_x(i).wait_send()
+        diagonal(i).wait_send()
 
     run(0, line, sent)
     for c in range(cuts):
         for copy in swap(c):
             copy.wait_send()
+
+
+def put_out(held, coh, held_out, coh_out, sems):
+    copies = [
+        pltpu.make_async_copy(held, held_out, sems.at[0]),
+        pltpu.make_async_copy(coh, coh_out, sems.at[1]),
+    ]
+    for copy in copies:
+        copy.start()
+    for copy in copies:
+        copy.wait()
 
 
 def on_device(capture, dropped):
@@ -510,7 +533,7 @@
     slot = [pltpu.VMEM((2, count, 2 * Q), jnp.bfloat16)] * 2
     slot = slot + [pltpu.VMEM((2, 2 * Q, 2 * LW), jnp.bfloat16)] * 2
     slot = slot + [pltpu.VMEM((2, Q, w), jnp.float32) for w in (2 * LW, LANES)]
-    held, coherent = pl.pallas_call(
+    results = pl.pallas_call(
         functools.partial(surfaces, slabs=slabs, groups=groups, own_bins=own_bins, own_w=own_w),
         out_shape=[
             jax.ShapeDtypeStruct((own_bins, own_w, LW), jnp.float32),
@@ -547,7 +570,14 @@
         ty,
         txs,
     )
-    return held, coherent
+    return pl.pallas_call(
+        put_out,
+        out_shape=[jax.ShapeDtypeStruct(r.shape, r.dtype) for r in results],
+        in_specs=[pl.BlockSpec(memory_space=pltpu.VMEM)] * 2,
+        out_specs=[pl.BlockSpec(memory_space=pltpu.HBM)] * 2,
+        scratch_shapes=[dma((2,))],
+        compiler_params=pltpu.CompilerParams(vmem_limit_bytes=2**20),
+    )(*results)
 
 
 def solution(mesh):

time: 37.5 us -> 34.1 us (0.909)
  local copies, waits for them, and re-layouts: 2.53 us -> 0.83 us
  Pallas kernels: 33.3 us -> 31.6 us
    pallas_call x1, Pallas kernels: 33.3 us -> 30.7 us  [on_device(): pl.pallas_call(functools.partial(surfaces, slabs=slabs, groups=groups, ow...]
    unnamed x4 -> x2, local copies, waits for them, and re-layouts: 2.53 us -> 0.83 us
    pallas_call x0 -> x1, Pallas kernels: none -> 0.9 us  [on_device(): pl.pallas_call(put_out, out_shape=[jax.ShapeDtypeStruct(r.shape, r.dtype)...]
where the time goes in v4:
time: 34.1 us; the launch traced here: 33.7 us
  Pallas kernels  31.6 us (93%)
  between operations  1.29 us (4%)
  local copies, waits for them, and re-layouts  0.83 us (2%)
    pallas_call x1, Pallas kernels, on_device(): pl.pallas_call(functools.partial(surfaces, slabs=slabs, groups=groups, ow...  30.7 us
    pallas_call x1, Pallas kernels, on_device(): pl.pallas_call(put_out, out_shape=[jax.ShapeDtypeStruct(r.shape, r.dtype)...  0.9 us
    unnamed x2, local copies, waits for them, and re-layouts  0.83 us

profile of v4, /device:TPU:0, one launch (start us, length us, event | category | flops | bytes accessed | tf_op | source)
XLA Modules:
  0.0 33.7 jit_solution(16250288639016466993)
XLA Ops:
  1.3 0.0 copy-start
  1.3 0.8 %copy-done = f32[2,8192]{1,0:T(2,128)S(1)} copy-done((f32[2,8192]{1,0:T(2,128)S(1)}, f32[2,8192]{1,0:T(2,128)}, u32[]{:S(2)}) %copy-start) | copy-done | bytes 65560
  2.1 30.7 %shard_map.77 = (f32[8,64,128]{2,1,0:T(8,128)S(1)}, f32[2,8,64,128]{3,2,1,0:T(8,128)S(1)}) custom-call(f32[64,2,128]{2,1,0:T(2,128)S(1)} %bitcast.3, s32[1]{0:T(128)S(6)} %copy.8.own_drop, bf16[2,512,256]{2,1,0:T(8,128)(2,1)} %constant.15.ty_hbm, bf16[2,512,256]{2,1,0:T(8,128)(2,1)} %constant.16.tx_hbm), custom_call_target="tpu_custom_call" | custom-call | tf_op jit(solution)/shard_map/pallas_call | solution.py:536
  32.8 0.9 %shard_map.78 = (f32[8,64,128]{2,1,0:T(8,128)}, f32[2,8,64,128]{3,2,1,0:T(8,128)}) custom-call(f32[8,64,128]{2,1,0:T(8,128)S(1)} %get-tuple-element.4.held, f32[2,8,64,128]{3,2,1,0:T(8,128)S(1)} %get-tuple-element.5.coh), custom_call_target="tpu_custom_call" | custom-call | tf_op jit(solution)/shard_map/pallas_call | solution.py:573
Async XLA Ops:
  1.3 0.8 %copy-start = (f32[2,8192]{1,0:T(2,128)S(1)}, f32[2,8192]{1,0:T(2,128)}, u32[]{:S(2)}) copy-start(f32[2,8192]{1,0:T(2,128)} %param.6) | copy-start | bytes 196612

commit v5 on v4

--- a/solution.py
+++ b/solution.py
@@ -63,8 +63,8 @@
     return cos_turns(turns & (period - 1), period), cos_turns((turns + period // 4) & (period - 1), period)
 
 def surfaces(
-    own_hbm, own_drop, ty_hbm, tx_hbm, held, coh,
-    raw, buf, infos, acc, got, ends, ty, txs, *rest,
+    raw, own_drop, ty_hbm, tx_hbm, held, coh,
+    buf, infos, acc, got, ends, ty, txs, *rest,
     slabs, groups, own_bins, own_w
 ):
     a_hi, a_lo, w_hi, w_lo, spec_y, spec_x = rest[:6]
@@ -92,8 +92,6 @@
     def load(src, dst, i):
         return pltpu.make_async_copy(src, dst, load_sem.at[i])
 
-    own_load = load(own_hbm, raw, 2)
-    own_load.start()
     tables = [load(ty_hbm, ty, 0), load(tx_hbm.at[grp], txs, 1)]
     for copy in tables:
         copy.start()
@@ -201,9 +199,6 @@
         base = ends[jnp.where(i == 0, z, before)] * jnp.where(i == 0, 0.0, 1.0)
         ends[z] = base + jnp.concatenate([total, total], axis=0) * jnp.where(down & (i > 0), -1.0, 1.0)
 
-    ends[...] = jnp.zeros_like(ends)
-    acc[...] = jnp.zeros_like(acc)
-    own_load.wait()
     for c in range(2):
         buf[place, grp, c * rows : (c + 1) * rows, :] = raw[:, c, :]
 
@@ -228,6 +223,8 @@
     to_x(0).start()
     to_y(0).start()
     run(1, line, lambda i: line_copy(i).start())
+    ends[...] = jnp.zeros_like(ends)
+    acc[...] = jnp.zeros_like(acc)
 
     lane = lax.broadcasted_iota(jnp.int32, (rows, LANES), 1)
     low = lane < HOP
@@ -244,34 +241,26 @@
     def spread(array, count):
         return jnp.concatenate([array] * count, axis=0)
 
-    def events(i, w):
-        if w == 0:
+    def events(i, w, end=False):
+        if end and w == 0:
             arrived(at_step(i), 1, 1)
-
-            @pl.when((i == 0) & (line > 1))
+        elif w == 0:
+            from_sides(i + 1)
+            reach(i + 1)
+        elif w == 2:
+            arrived(at_step(i), 1, 1)
+        elif w == 3:
+
+            @pl.when(i + 3 < line)
             def _():
-                from_sides(i + 1)
-
-        elif w == 2:
-
-            @pl.when(i + 1 < line)
-            def _():
-                reach(i + 1)
-
-        else:
-            j = 2 * i + (w + 1) // 2
-
-            @pl.when(j + 2 < line)
-            def _():
-                from_line(j + 2)
-
-            @pl.when((j > 1) & (j < line))
-            def _():
-                from_sides(j)
+                from_line(i + 3)
 
     def locate(u):
-        z = at_step(u // 4)
-        n = 4 * z + 2 * ((chip + u // 2) % 2) + core
+        h = u // 2
+        far = ((h % 2 == 0) & (h > 0)) | (h == 2 * line - 1)
+        i = jnp.where(far, (h - 1) // 2, (h + 1) // 2)
+        z = at_step(i)
+        n = 4 * z + 2 * ((chip + far.astype(jnp.int32)) % 2) + core
         return z, n, n // 2, 1 - u % 2
 
     def analyze(u, slot, first=False):
@@ -390,10 +379,10 @@
 
     units = 4 * line
 
-    def step(i, w, slot):
+    def step(i, w, slot, end=False):
         u = 4 * i + w
         slot = u % 2
-        events(i, w)
+        events(i, w, end)
         accumulate(slot, 0, 0)
         turned = build(u + 1, 1 - slot)
         finish = analyze(u + 2, slot)
@@ -410,6 +399,13 @@
             slot = step(i, w, slot)
         return slot
 
+    if line > 1:
+        from_line(zero + 1)
+    from_sides(zero)
+    for copy in tables:
+        copy.wait()
+    analyze(zero, 0, True)()
+
     @pl.when(grp != last)
     def _():
         to_group.wait_recv()
@@ -417,22 +413,16 @@
 
     info_copy(slab + 1 - 2 * core, 1, 0, 1, partner).wait_recv()
     others(lambda p, i: to_chip(p, i).start())
-    for copy in tables:
-        copy.wait()
-    if line > 1:
-        from_line(zero + 1)
-    from_sides(zero)
-    analyze(zero, 0, True)()
-    reach(zero)
     if line > 2:
         from_line(zero + 2)
+    reach(zero)
     turned = build(zero, 0, True)
     analyze(zero + 1, 1)()
     for c in range(2 * cuts):
         turned(c)
     slot = lax.fori_loop(0, line - 1, steps, zero)
-    slot = step(zero + line - 1, 0, slot)
-    step(zero + line - 1, 1, slot)
+    slot = step(zero + line - 1, 0, slot, True)
+    step(zero + line - 1, 1, slot, True)
     slot = 0
     turned = build(zero + units - 1, 1 - slot)
     for c in range(2 * cuts):
@@ -539,10 +529,9 @@
             jax.ShapeDtypeStruct((own_bins, own_w, LW), jnp.float32),
             jax.ShapeDtypeStruct((2, own_bins, own_w, LW), jnp.float32),
         ],
-        in_specs=[pl.BlockSpec(memory_space=space) for space in (pltpu.HBM, pltpu.SMEM, pltpu.HBM, pltpu.HBM)],
+        in_specs=[pl.BlockSpec(memory_space=space) for space in (pltpu.VMEM, pltpu.SMEM, pltpu.HBM, pltpu.HBM)],
         out_specs=[pl.BlockSpec(memory_space=pltpu.VMEM)] * 2,
         scratch_shapes=[
-            pltpu.VMEM((local, 2, LANES), jnp.float32),
             pltpu.VMEM((slabs // 2, groups, 2 * local, LANES), jnp.float32),
             pltpu.VMEM((slabs, 8, LANES), jnp.float32),
             pltpu.VMEM((2, 3, own_bins, own_w, LW), jnp.float32),
@@ -559,7 +548,7 @@
             dma((slabs // 2 + 1,)),
             dma((slabs // 2 + 2,)),
             dma((2, 3 * own_bins)),
-            dma((3,)),
+            dma((2,)),
         ],
         compiler_params=pltpu.CompilerParams(
             collective_id=0, has_side_effects=True, vmem_limit_bytes=VMEM_LIMIT

time: 34.1 us -> 33.2 us (0.974)
  Pallas kernels: 31.6 us -> 30.8 us
    pallas_call x1, Pallas kernels: 30.7 us -> 29.9 us  [on_device(): pl.pallas_call(functools.partial(surfaces, slabs=slabs, groups=groups, ow...]
where the time goes in v5:
time: 33.2 us; the launch traced here: 32.9 us
  Pallas kernels  30.8 us (93%)
  between operations  1.29 us (4%)
  local copies, waits for them, and re-layouts  0.83 us (2%)
    pallas_call x1, Pallas kernels, on_device(): pl.pallas_call(functools.partial(surfaces, slabs=slabs, groups=groups, ow...  29.9 us
    pallas_call x1, Pallas kernels, on_device(): pl.pallas_call(put_out, out_shape=[jax.ShapeDtypeStruct(r.shape, r.dtype)...  0.9 us
    unnamed x2, local copies, waits for them, and re-layouts  0.83 us

profile of v5, /device:TPU:0, one launch (start us, length us, event | category | flops | bytes accessed | tf_op | source)
XLA Modules:
  0.0 32.9 jit_solution(9581111533661415710)
XLA Ops:
  1.3 0.0 copy-start
  1.3 0.8 %copy-done = f32[2,8192]{1,0:T(2,128)S(1)} copy-done((f32[2,8192]{1,0:T(2,128)S(1)}, f32[2,8192]{1,0:T(2,128)}, u32[]{:S(2)}) %copy-start) | copy-done | bytes 65560
  2.1 29.9 %shard_map.77 = (f32[8,64,128]{2,1,0:T(8,128)S(1)}, f32[2,8,64,128]{3,2,1,0:T(8,128)S(1)}) custom-call(f32[64,2,128]{2,1,0:T(2,128)S(1)} %bitcast.3, s32[1]{0:T(128)S(6)} %copy.8.own_drop, bf16[2,512,256]{2,1,0:T(8,128)(2,1)} %constant.15.ty_hbm, bf16[2,512,256]{2,1,0:T(8,128)(2,1)} %constant.16.tx_hbm), custom_call_target="tpu_custom_call" | custom-call | tf_op jit(solution)/shard_map/pallas_call | solution.py:526
  32.0 0.9 %shard_map.78 = (f32[8,64,128]{2,1,0:T(8,128)}, f32[2,8,64,128]{3,2,1,0:T(8,128)}) custom-call(f32[8,64,128]{2,1,0:T(8,128)S(1)} %get-tuple-element.4.held, f32[2,8,64,128]{3,2,1,0:T(8,128)S(1)} %get-tuple-element.5.coh), custom_call_target="tpu_custom_call" | custom-call | tf_op jit(solution)/shard_map/pallas_call | solution.py:562
Async XLA Ops:
  1.3 0.8 %copy-start = (f32[2,8192]{1,0:T(2,128)S(1)}, f32[2,8192]{1,0:T(2,128)}, u32[]{:S(2)}) copy-start(f32[2,8192]{1,0:T(2,128)} %param.6) | copy-start | bytes 196612

commit v6 on v5

--- a/solution.py
+++ b/solution.py
@@ -64,7 +64,7 @@
 
 def surfaces(
     raw, own_drop, ty_hbm, tx_hbm, held, coh,
-    buf, infos, acc, got, ends, ty, txs, *rest,
+    buf, infos, acc, got, ends, phases, turns, ty, txs, *rest,
     slabs, groups, own_bins, own_w
 ):
     a_hi, a_lo, w_hi, w_lo, spec_y, spec_x = rest[:6]
@@ -146,8 +146,16 @@
     def info_arrived(p):
         info_copy(2 * p, 2, 0, 2 + p, partner).wait_recv()
 
-    def line_copy(i):
-        return moved(level, 0, 0, line_sem.at[i], (slab + 4 * (at_step(i) - level), grp))
+    def line_copy(z):
+        return moved(level, 0, 0, line_sem.at[z], (slab + 4 * (z - level), grp))
+
+    def lines(d):
+        for z in (level - d, level + d):
+
+            @pl.when((z >= 0) & (z < line))
+            def _():
+                line_copy(z).start()
+
 
     def to_x(i):
         return moved(at_step(i), 0, 0, x_sem.at[i], beside)
@@ -222,7 +230,7 @@
 
     to_x(0).start()
     to_y(0).start()
-    run(1, line, lambda i: line_copy(i).start())
+    run(1, line, lines)
     ends[...] = jnp.zeros_like(ends)
     acc[...] = jnp.zeros_like(acc)
 
@@ -300,22 +308,31 @@
 
         return finish
 
-    def build(u, slot, first=False):
+    def build(u, slot, fresh, first=False):
         z, n, at, g = locate(u)
-        if first:
-            rel = infos[slab, 4:8, :] * jnp.where(core > 0, 1.0, 0.0)
-            rel = jnp.concatenate([rel, rel], axis=0)
-        else:
-            rel = ends[z]
-            for k in range(1, 4):
-                drop = infos[4 * z + k, 4:8, :] * jnp.where(4 * z + k > n, 1.0, 0.0)
-                rel = rel - jnp.concatenate([drop, drop], axis=0)
-        stamp = rel.astype(jnp.int32)
-        t = (spread(stamp, 2) + HOP * jlane) & (period - 1)
-        phq = rotation((turn * t) & (2 * period - 1), 2 * period)
-        phx = [rotation(kchan * ((stamp + HOP * (jsub + p)) & (NCH - 1)), NCH) for p in range(2)]
-        phy = [rotation(lchan * ((stamp + HOP * (jsub + p)) & (NCH - 1)), NCH) for p in range(2)]
-
+        if fresh:
+            if first:
+                rel = infos[slab, 4:8, :] * jnp.where(core > 0, 1.0, 0.0)
+                rel = jnp.concatenate([rel, rel], axis=0)
+            else:
+                rel = ends[z]
+                for k in range(1, 4):
+                    drop = infos[4 * z + k, 4:8, :] * jnp.where(4 * z + k > n, 1.0, 0.0)
+                    rel = rel - jnp.concatenate([drop, drop], axis=0)
+            stamp = rel.astype(jnp.int32)
+            t = (spread(stamp, 2) + HOP * jlane) & (period - 1)
+            phq = rotation((turn * t) & (2 * period - 1), 2 * period)
+            phx = [rotation(kchan * ((stamp + HOP * (jsub + p)) & (NCH - 1)), NCH) for p in range(2)]
+            phy = [rotation(lchan * ((stamp + HOP * (jsub + p)) & (NCH - 1)), NCH) for p in range(2)]
+            for p in range(2):
+                for k in range(2):
+                    phases[4 * p + k] = phx[p][k] * (ksign if k else 1.0)
+                    phases[4 * p + 2 + k] = phy[p][k]
+            turns[0] = phq[0]
+            turns[1] = phq[1]
+        phx = [(phases[4 * p], phases[4 * p + 1]) for p in range(2)]
+        phy = [(phases[4 * p + 2], phases[4 * p + 3]) for p in range(2)]
+        phq = turns[0], turns[1]
         zrs, zis, kxs = [], [], []
         for p in range(2):
             c, s = (spread(v, rows // 8) for v in phy[p])
@@ -323,7 +340,7 @@
             yr, yi = part[:, :LW], part[:, LW:]
             zrs.append(yr * c - yi * s)
             zis.append(yr * s + yi * c)
-            c, s = spread(phx[p][0], rows // 8), spread(phx[p][1] * ksign, rows // 8)
+            c, s = spread(phx[p][0], rows // 8), spread(phx[p][1], rows // 8)
             part = spec_x[slot, p * rows : (p + 1) * rows, :]
             kxs.append(part * c + pltpu.roll(part, own_w, 1) * s)
         zr_hi, zr_lo = split(jnp.concatenate(zrs, axis=0))
@@ -384,7 +401,7 @@
         slot = u % 2
         events(i, w, end)
         accumulate(slot, 0, 0)
-        turned = build(u + 1, 1 - slot)
+        turned = build(u + 1, 1 - slot, w % 2 == 1)
         finish = analyze(u + 2, slot)
         turned(0)
         for c in range(1, 2 * cuts):
@@ -416,7 +433,7 @@
     if line > 2:
         from_line(zero + 2)
     reach(zero)
-    turned = build(zero, 0, True)
+    turned = build(zero, 0, True, True)
     analyze(zero + 1, 1)()
     for c in range(2 * cuts):
         turned(c)
@@ -424,7 +441,7 @@
     slot = step(zero + line - 1, 0, slot, True)
     step(zero + line - 1, 1, slot, True)
     slot = 0
-    turned = build(zero + units - 1, 1 - slot)
+    turned = build(zero + units - 1, 1 - slot, False)
     for c in range(2 * cuts):
         turned(c)
     def swap(c):
@@ -474,7 +491,7 @@
 
     to_partner.wait_send()
     others(lambda p, i: to_chip(p, i).wait_send())
-    run(1, line, lambda i: line_copy(i).wait_send())
+    run(1, line, lambda i: line_copy((level + i) % line).wait_send())
 
     def sent(i):
         to_x(i).wait_send()
@@ -537,6 +554,8 @@
             pltpu.VMEM((2, 3, own_bins, own_w, LW), jnp.float32),
             pltpu.VMEM((3, own_bins, own_w, LW), jnp.float32),
             pltpu.VMEM((line, 8, LANES), jnp.float32),
+            pltpu.VMEM((8, 8, LANES), jnp.float32),
+            pltpu.VMEM((2, 16, LANES), jnp.float32),
             pltpu.VMEM(ty.shape, jnp.bfloat16),
             pltpu.VMEM(txs.shape[1:], jnp.bfloat16),
             *slot,

time: 33.2 us -> 33.2 us (level)
  no operation moved by 1% of the time
where the time goes in v6:
time: 33.2 us; the launch traced here: 32.8 us
  Pallas kernels  30.7 us (92%)
  between operations  1.29 us (4%)
  local copies, waits for them, and re-layouts  0.83 us (2%)
    pallas_call x1, Pallas kernels, on_device(): pl.pallas_call(functools.partial(surfaces, slabs=slabs, groups=groups, ow...  29.8 us
    pallas_call x1, Pallas kernels, on_device(): pl.pallas_call(put_out, out_shape=[jax.ShapeDtypeStruct(r.shape, r.dtype)...  0.9 us
    unnamed x2, local copies, waits for them, and re-layouts  0.83 us

profile of v6, /device:TPU:0, one launch (start us, length us, event | category | flops | bytes accessed | tf_op | source)
XLA Modules:
  0.0 32.8 jit_solution(6564320516046311026)
XLA Ops:
  1.3 0.0 copy-start
  1.3 0.8 %copy-done = f32[2,8192]{1,0:T(2,128)S(1)} copy-done((f32[2,8192]{1,0:T(2,128)S(1)}, f32[2,8192]{1,0:T(2,128)}, u32[]{:S(2)}) %copy-start) | copy-done | bytes 65560
  2.1 29.8 %shard_map.77 = (f32[8,64,128]{2,1,0:T(8,128)S(1)}, f32[2,8,64,128]{3,2,1,0:T(8,128)S(1)}) custom-call(f32[64,2,128]{2,1,0:T(2,128)S(1)} %bitcast.3, s32[1]{0:T(128)S(6)} %copy.8.own_drop, bf16[2,512,256]{2,1,0:T(8,128)(2,1)} %constant.15.ty_hbm, bf16[2,512,256]{2,1,0:T(8,128)(2,1)} %constant.16.tx_hbm), custom_call_target="tpu_custom_call" | custom-call | tf_op jit(solution)/shard_map/pallas_call | solution.py:543
  31.9 0.9 %shard_map.78 = (f32[8,64,128]{2,1,0:T(8,128)}, f32[2,8,64,128]{3,2,1,0:T(8,128)}) custom-call(f32[8,64,128]{2,1,0:T(8,128)S(1)} %get-tuple-element.4.held, f32[2,8,64,128]{3,2,1,0:T(8,128)S(1)} %get-tuple-element.5.coh), custom_call_target="tpu_custom_call" | custom-call | tf_op jit(solution)/shard_map/pallas_call | solution.py:581
Async XLA Ops:
  1.3 0.8 %copy-start = (f32[2,8192]{1,0:T(2,128)S(1)}, f32[2,8192]{1,0:T(2,128)}, u32[]{:S(2)}) copy-start(f32[2,8192]{1,0:T(2,128)} %param.6) | copy-start | bytes 196612

commit v7 on v6

--- a/solution.py
+++ b/solution.py
@@ -416,17 +416,17 @@
             slot = step(i, w, slot)
         return slot
 
+    @pl.when(grp != last)
+    def _():
+        to_group.wait_recv()
+        to_partner.start()
+
     if line > 1:
         from_line(zero + 1)
     from_sides(zero)
     for copy in tables:
         copy.wait()
     analyze(zero, 0, True)()
-
-    @pl.when(grp != last)
-    def _():
-        to_group.wait_recv()
-        to_partner.start()
 
     info_copy(slab + 1 - 2 * core, 1, 0, 1, partner).wait_recv()
     others(lambda p, i: to_chip(p, i).start())

time: 33.2 us -> 33.2 us (level)
  no operation moved by 1% of the time
where the time goes in v7:
time: 33.2 us; the launch traced here: 32.9 us
  Pallas kernels  30.8 us (93%)
  between operations  1.29 us (4%)
  local copies, waits for them, and re-layouts  0.83 us (2%)
    pallas_call x1, Pallas kernels, on_device(): pl.pallas_call(functools.partial(surfaces, slabs=slabs, groups=groups, ow...  29.9 us
    pallas_call x1, Pallas kernels, on_device(): pl.pallas_call(put_out, out_shape=[jax.ShapeDtypeStruct(r.shape, r.dtype)...  0.9 us
    unnamed x2, local copies, waits for them, and re-layouts  0.83 us

profile of v7, /device:TPU:0, one launch (start us, length us, event | category | flops | bytes accessed | tf_op | source)
XLA Modules:
  0.0 32.9 jit_solution(10283832545106348609)
XLA Ops:
  1.3 0.0 copy-start
  1.3 0.8 %copy-done = f32[2,8192]{1,0:T(2,128)S(1)} copy-done((f32[2,8192]{1,0:T(2,128)S(1)}, f32[2,8192]{1,0:T(2,128)}, u32[]{:S(2)}) %copy-start) | copy-done | bytes 65560
  2.1 29.9 %shard_map.77 = (f32[8,64,128]{2,1,0:T(8,128)S(1)}, f32[2,8,64,128]{3,2,1,0:T(8,128)S(1)}) custom-call(f32[64,2,128]{2,1,0:T(2,128)S(1)} %bitcast.3, s32[1]{0:T(128)S(6)} %copy.8.own_drop, bf16[2,512,256]{2,1,0:T(8,128)(2,1)} %constant.15.ty_hbm, bf16[2,512,256]{2,1,0:T(8,128)(2,1)} %constant.16.tx_hbm), custom_call_target="tpu_custom_call" | custom-call | tf_op jit(solution)/shard_map/pallas_call | solution.py:543
  32.0 0.9 %shard_map.78 = (f32[8,64,128]{2,1,0:T(8,128)}, f32[2,8,64,128]{3,2,1,0:T(8,128)}) custom-call(f32[8,64,128]{2,1,0:T(8,128)S(1)} %get-tuple-element.4.held, f32[2,8,64,128]{3,2,1,0:T(8,128)S(1)} %get-tuple-element.5.coh), custom_call_target="tpu_custom_call" | custom-call | tf_op jit(solution)/shard_map/pallas_call | solution.py:581
Async XLA Ops:
  1.3 0.8 %copy-start = (f32[2,8192]{1,0:T(2,128)S(1)}, f32[2,8192]{1,0:T(2,128)}, u32[]{:S(2)}) copy-start(f32[2,8192]{1,0:T(2,128)} %param.6) | copy-start | bytes 196612
